TPU v7x, 256 devices: a whole 4x4x8 slice. The times are simulated.
256 devices in a mesh: row: 8 (over x, y_hi), col: 32 (over z, y_lo, core).
Axes of the slice: x: 4, y: 4 (y_hi: 2, y_lo: 2; y = y_hi * 2 + y_lo), z: 8, core: 2. Of those that a mesh axis runs over, the one named last changes fastest.
Arguments:
- e_field: float32 [3, 64, 64, 4096], P(None, None, 'row', 'col'), may hold values from -6 to 6
- h_field: float32 [3, 64, 64, 4096], P(None, None, 'row', 'col'), may hold values from -6 to 6
- e_coef: float32 [64, 64, 4096], P(None, 'row', 'col'), may hold values from 0.125 to 0.5
- basis: float32 [128, 64, 4096], P('row', None, 'col'), may hold values from -0.01171875 to 0.01171875
- pml_width: int32 [4], replicated, may hold values from 2 to 8
- snap_index: int32 [64], replicated, may hold values from 0 to 383
Outputs:
- e_final: float32 [3, 64, 64, 4096], P(None, None, 'row', 'col')
- h_final: float32 [3, 64, 64, 4096], P(None, None, 'row', 'col')
- coefficients: float32 [64, 128], replicated
- gram: float32 [64, 64], replicated
All inputs are finite; a program needn't handle non-finite values.
Results may differ from a plain program's by a relative error of at most 0.00008.
Values sent between devices are 32-bit elements; how exact they have to be, the bound alone decides.
A program may use at most 64 MiB of HBM per device.

v0:
```python
import jax
import jax.numpy as jnp
from jax import lax
from jax.sharding import Mesh
from jax.sharding import PartitionSpec as P

STEPS = 8
ROW = ("row_0", "row_1")
COL = ("col_0", "col_1", "col_2")
ROW_COL = ("row_0", "row_1", "col_0", "col_1", "col_2")


time_step = 0.5
sigma_top = 4.0
alpha_shift = 0.05


def from_behind(block, axis, distance):
    devices = range(lax.axis_size(axis))
    route = [(i - distance, i) for i in devices if i - distance in devices]
    return lax.ppermute(block, axis, route)


def by_axis(array, axes):
    for axis in axes:
        array = lax.psum(array, axis)
    return array


def forward(field, axis, plane):
    count = field.shape[axis]
    after = jnp.concatenate(
        [lax.slice_in_dim(field, 1, count, axis=axis), jnp.expand_dims(plane, axis)], axis
    )
    return after - field


def backward(field, axis, plane):
    count = field.shape[axis]
    before = jnp.concatenate(
        [jnp.expand_dims(plane, axis), lax.slice_in_dim(field, 0, count - 1, axis=axis)], axis
    )
    return field - before


def absorber(positions, total, low, high):
    depth = jnp.maximum(
        jnp.maximum((low - positions) / low, (positions - (total - 1.0 - high)) / high), 0.0
    )
    sigma = sigma_top * depth**3
    damp = jnp.exp(-(sigma + alpha_shift) * time_step)
    gain = sigma / (sigma + alpha_shift) * (damp - 1.0)
    return (damp, gain)


def magnetic(e_field, h_field, psi, next_x, next_y, damp_x, gain_x, damp_y, gain_y):
    e_x, e_y, e_z = (e_field[0], e_field[1], e_field[2])
    h_x, h_y, h_z = (h_field[0], h_field[1], h_field[2])
    zplane = jnp.zeros_like(e_x[0])
    ez_dy = forward(e_z, 2, next_y[1])
    ey_dz = forward(e_y, 0, zplane)
    ex_dz = forward(e_x, 0, zplane)
    ez_dx = forward(e_z, 1, next_x[1])
    ey_dx = forward(e_y, 1, next_x[0])
    ex_dy = forward(e_x, 2, next_y[0])
    psi_hxy = damp_y * psi[0] + gain_y * ez_dy
    psi_hyx = damp_x * psi[1] + gain_x * ez_dx
    psi_hzx = damp_x * psi[2] + gain_x * ey_dx
    psi_hzy = damp_y * psi[3] + gain_y * ex_dy
    h_x = h_x - time_step * (ez_dy + psi_hxy - ey_dz)
    h_y = h_y - time_step * (ex_dz - ez_dx - psi_hyx)
    h_z = h_z - time_step * (ey_dx + psi_hzx - ex_dy - psi_hzy)
    return (jnp.stack((h_x, h_y, h_z)), (psi_hxy, psi_hyx, psi_hzx, psi_hzy))


def electric(e_field, h_field, psi, e_coef, prev_x, prev_y, damp_x, gain_x, damp_y, gain_y):
    e_x, e_y, e_z = (e_field[0], e_field[1], e_field[2])
    h_x, h_y, h_z = (h_field[0], h_field[1], h_field[2])
    zplane = jnp.zeros_like(h_x[0])
    hz_dy = backward(h_z, 2, prev_y[1])
    hy_dz = backward(h_y, 0, zplane)
    hx_dz = backward(h_x, 0, zplane)
    hz_dx = backward(h_z, 1, prev_x[1])
    hy_dx = backward(h_y, 1, prev_x[0])
    hx_dy = backward(h_x, 2, prev_y[0])
    psi_exy = damp_y * psi[0] + gain_y * hz_dy
    psi_eyx = damp_x * psi[1] + gain_x * hz_dx
    psi_ezx = damp_x * psi[2] + gain_x * hy_dx
    psi_ezy = damp_y * psi[3] + gain_y * hx_dy
    e_x = e_x + e_coef * (hz_dy + psi_exy - hy_dz)
    e_y = e_y + e_coef * (hx_dz - hz_dx - psi_eyx)
    e_z = e_z + e_coef * (hy_dx + psi_ezx - hx_dy - psi_ezy)
    return (jnp.stack((e_x, e_y, e_z)), (psi_exy, psi_eyx, psi_ezx, psi_ezy))


def shards(e_field, h_field, e_coef, basis, pml_width, snap_index):
    depth_z, rows_here, cols_here = e_coef.shape
    full_x = rows_here * lax.axis_size(ROW)
    full_y = cols_here * lax.axis_size(COL)
    x_first = lax.axis_index(ROW) * rows_here
    y_first = lax.axis_index(COL) * cols_here
    widths = pml_width.astype(jnp.float32)
    x_pos = x_first.astype(jnp.float32) + jnp.arange(rows_here, dtype=jnp.float32)
    y_pos = y_first.astype(jnp.float32) + jnp.arange(cols_here, dtype=jnp.float32)
    hdx, hgx = absorber(x_pos + 0.5, float(full_x), widths[0], widths[1])
    hdy, hgy = absorber(y_pos + 0.5, float(full_y), widths[2], widths[3])
    edx, egx = absorber(x_pos, float(full_x), widths[0], widths[1])
    edy, egy = absorber(y_pos, float(full_y), widths[2], widths[3])
    hdx, hgx, edx, egx = [v.reshape(1, rows_here, 1) for v in (hdx, hgx, edx, egx)]
    hdy, hgy, edy, egy = [v.reshape(1, 1, cols_here) for v in (hdy, hgy, edy, egy)]
    zeros_cells = jnp.zeros((depth_z, rows_here, cols_here), jnp.float32)
    psi_mag = (zeros_cells,) * 4
    psi_ele = (zeros_cells,) * 4
    for step in range(STEPS):
        next_x = from_behind(e_field[1:3, :, 0, :], ROW, -1)
        next_y = from_behind(jnp.stack((e_field[0, :, :, 0], e_field[2, :, :, 0])), COL, -1)
        h_field, psi_mag = magnetic(e_field, h_field, psi_mag, next_x, next_y, hdx, hgx, hdy, hgy)
        prev_x = from_behind(h_field[1:3, :, -1, :], ROW, 1)
        prev_y = from_behind(jnp.stack((h_field[0, :, :, -1], h_field[2, :, :, -1])), COL, 1)
        e_field, psi_ele = electric(
            e_field, h_field, psi_ele, e_coef, prev_x, prev_y, edx, egx, edy, egy
        )
    planes = jnp.concatenate((e_field, h_field), 0).reshape(6 * depth_z, rows_here, cols_here)
    snaps = jnp.take(planes, snap_index, axis=0)
    count = snaps.shape[0]
    flat = snaps.reshape(count, rows_here * cols_here)
    gram_part = jnp.dot(flat, flat.T, precision=lax.Precision.HIGHEST) / float(full_x * full_y)
    local_modes = lax.all_to_all(basis, ROW, split_axis=1, concat_axis=0, tiled=True)
    coef_part = jnp.dot(
        flat, local_modes.reshape(local_modes.shape[0], -1).T, precision=lax.Precision.HIGHEST
    )
    coefficients, gram = (by_axis(coef_part, ROW_COL), by_axis(gram_part, ROW_COL))
    return (e_field, h_field, coefficients, gram)


def solution(mesh):
    split = Mesh(mesh.devices.reshape(4, 2, 8, 2, 2), ("row_0", "row_1", "col_0", "col_1", "col_2"))
    return jax.shard_map(
        shards,
        mesh=split,
        in_specs=(
            P(None, None, ROW, COL),
            P(None, None, ROW, COL),
            P(None, ROW, COL),
            P(ROW, None, COL),
            P(),
            P(),
        ),
        out_specs=(P(None, None, ROW, COL), P(None, None, ROW, COL), P(), P()),
        check_vma=False,
    )
```

profile of v0, /device:TPU:1, one launch (start us, length us, event | category | flops | bytes accessed | tf_op | source)
XLA Modules:
  0.0 416.5 jit_solution(7778291619104819544)
XLA Ops:
  4.5 5.1 %collective-permute-start.1 = (f32[2,64,8]{1,2,0:T(8,128)S(1)}, f32[2,64,8]{1,2,0:T(8,128)S(1)}, u32[]{:S(2)}, u32[]{:S(2)}) collective-permute-start(f32[2,64,8]{1,2,0:T(8,128)S(1)} %pad_maximum_fusion.17), channel_id=1, source_target_pairs={{1,0},{2,1},{3,2},{4,3},{5,4},{6,5},{7,6},{8,7},{9,8},{10,9},{11,1... | collective-permute-start | bytes 12296 | tf_op jit(solution)/shard_map/ppermute | solution.py:21
  10.7 6.4 %all-to-all-start = ((f32[16,64,128]{2,0,1:T(8,128)}), f32[16,64,128]{2,0,1:T(8,128)}, u32[]{:S(2)}, u32[]{:S(2)}) async-start(f32[16,64,128]{2,0,1:T(8,128)} %copy.1592), calls=%async_computation | async-start | bytes 1048576 | tf_op jit(solution)/shard_map/all_to_all | solution.py:128
  31.1 2.2 bitcast_subtract_fusion.1
  33.6 3.4 collective-permute-start.2
  37.0 2.0 bitcast_subtract_fusion
  39.9 5.7 %collective-permute-start.3 = (f32[2,64,128]{2,1,0:T(8,128)S(1)}, f32[2,64,128]{2,1,0:T(8,128)S(1)}, u32[]{:S(2)}, u32[]{:S(2)}) collective-permute-start(f32[2,64,128]{2,1,0:T(8,128)S(1)} %bitcast.519), channel_id=1, source_target_pairs={{0,32},{32,64},{64,96},{96,128},{128,160},{160,192},{192,224},{1,3... | collective-permute-start | bytes 196616 | tf_op jit(solution)/shard_map/ppermute | solution.py:21
  48.0 2.0 multiply_add_fusion.69
  50.2 1.9 collective-permute-start.5
  59.0 3.7 collective-permute-done.4
  62.6 2.3 multiply_subtract_fusion.20
  65.2 2.4 multiply_subtract_fusion.19
  67.9 4.8 %collective-permute-start.6 = (f32[2,64,8]{1,2,0:T(8,128)S(1)}, f32[2,64,8]{1,2,0:T(8,128)S(1)}, u32[]{:S(2)}, u32[]{:S(2)}) collective-permute-start(f32[2,64,8]{1,2,0:T(8,128)S(1)} %pad_maximum_fusion.20), channel_id=1, source_target_pairs={{0,1},{1,2},{2,3},{3,4},{4,5},{5,6},{6,7},{7,8},{8,9},{9,10},{10,1... | collective-permute-start | bytes 12296 | tf_op jit(solution)/shard_map/ppermute | solution.py:21
  74.1 5.9 %collective-permute-start.7 = (f32[2,64,128]{2,1,0:T(8,128)}, f32[2,64,128]{2,1,0:T(8,128)}, u32[]{:S(2)}, u32[]{:S(2)}) collective-permute-start(f32[2,64,128]{2,1,0:T(8,128)} %fusion.15), channel_id=1, source_target_pairs={{0,32},{32,64},{64,96},{96,128},{128,160},{160,192},{192,224},{1,3... | collective-permute-start | bytes 196616 | tf_op jit(solution)/shard_map/ppermute | solution.py:21
  85.2 2.0 multiply_add_fusion.55
  88.0 1.9 collective-permute-start.9
  101.2 2.3 multiply_subtract_fusion.17
  104.5 5.1 %collective-permute-start.10 = (f32[2,64,8]{1,2,0:T(8,128)S(1)}, f32[2,64,8]{1,2,0:T(8,128)S(1)}, u32[]{:S(2)}, u32[]{:S(2)}) collective-permute-start(f32[2,64,8]{1,2,0:T(8,128)S(1)} %pad_maximum_fusion.22), channel_id=1, source_target_pairs={{0,1},{1,2},{2,3},{3,4},{4,5},{5,6},{6,7},{7,8},{8,9},{9,10},{10,1... | collective-permute-start | bytes 12296 | tf_op jit(solution)/shard_map/ppermute | solution.py:21
  109.6 2.2 multiply_subtract_fusion.15
  113.2 4.9 %collective-permute-start.11 = (f32[2,64,128]{2,1,0:T(8,128)}, f32[2,64,128]{2,1,0:T(8,128)}, u32[]{:S(2)}, u32[]{:S(2)}) collective-permute-start(f32[2,64,128]{2,1,0:T(8,128)} %bitcast.74), channel_id=1, source_target_pairs={{0,32},{32,64},{64,96},{96,128},{128,160},{160,192},{192,224},{1,3... | collective-permute-start | bytes 196616 | tf_op jit(solution)/shard_map/ppermute | solution.py:21
  127.8 1.9 collective-permute-start.13
  136.6 2.3 multiply_subtract_fusion.13
  142.2 2.3 multiply_subtract_fusion.14
  145.5 5.0 %collective-permute-start.14 = (f32[2,64,8]{1,2,0:T(8,128)S(1)}, f32[2,64,8]{1,2,0:T(8,128)S(1)}, u32[]{:S(2)}, u32[]{:S(2)}) collective-permute-start(f32[2,64,8]{1,2,0:T(8,128)S(1)} %pad_maximum_fusion.24), channel_id=1, source_target_pairs={{0,1},{1,2},{2,3},{3,4},{4,5},{5,6},{6,7},{7,8},{8,9},{9,10},{10,1... | collective-permute-start | bytes 12296 | tf_op jit(solution)/shard_map/ppermute | solution.py:21
  153.2 5.6 %collective-permute-start.15 = (f32[2,64,128]{2,1,0:T(8,128)}, f32[2,64,128]{2,1,0:T(8,128)}, u32[]{:S(2)}, u32[]{:S(2)}) collective-permute-start(f32[2,64,128]{2,1,0:T(8,128)} %fusion.12), channel_id=1, source_target_pairs={{0,32},{32,64},{64,96},{96,128},{128,160},{160,192},{192,224},{1,3... | collective-permute-start | bytes 196616 | tf_op jit(solution)/shard_map/ppermute | solution.py:21
  158.8 2.0 copy.1593
  161.7 2.1 multiply_add_fusion.38
  181.6 2.4 multiply_subtract_fusion.11
  185.0 5.2 %collective-permute-start.18 = (f32[2,64,8]{1,2,0:T(8,128)S(1)}, f32[2,64,8]{1,2,0:T(8,128)S(1)}, u32[]{:S(2)}, u32[]{:S(2)}) collective-permute-start(f32[2,64,8]{1,2,0:T(8,128)S(1)} %pad_maximum_fusion.26), channel_id=1, source_target_pairs={{0,1},{1,2},{2,3},{3,4},{4,5},{5,6},{6,7},{7,8},{8,9},{9,10},{10,1... | collective-permute-start | bytes 12296 | tf_op jit(solution)/shard_map/ppermute | solution.py:21
  190.2 2.1 multiply_subtract_fusion.9
  193.2 4.4 %collective-permute-start.19 = (f32[2,64,128]{2,1,0:T(8,128)S(1)}, f32[2,64,128]{2,1,0:T(8,128)}, u32[]{:S(2)}, u32[]{:S(2)}) collective-permute-start(f32[2,64,128]{2,1,0:T(8,128)S(1)} %bitcast.521), channel_id=1, source_target_pairs={{0,32},{32,64},{64,96},{96,128},{128,160},{160,192},{192,224},{1,3... | collective-permute-start | bytes 196616 | tf_op jit(solution)/shard_map/ppermute | solution.py:21
  204.3 2.0 multiply_add_fusion.22
  217.6 2.1 multiply_subtract_fusion.7
  223.1 2.3 multiply_subtract_fusion.8
  227.2 4.8 %collective-permute-start.22 = (f32[2,64,8]{1,2,0:T(8,128)S(1)}, f32[2,64,8]{1,2,0:T(8,128)S(1)}, u32[]{:S(2)}, u32[]{:S(2)}) collective-permute-start(f32[2,64,8]{1,2,0:T(8,128)S(1)} %pad_maximum_fusion.28), channel_id=1, source_target_pairs={{0,1},{1,2},{2,3},{3,4},{4,5},{5,6},{6,7},{7,8},{8,9},{9,10},{10,1... | collective-permute-start | bytes 12296 | tf_op jit(solution)/shard_map/ppermute | solution.py:21
  234.6 5.8 %collective-permute-start.23 = (f32[2,64,128]{2,1,0:T(8,128)}, f32[2,64,128]{2,1,0:T(8,128)}, u32[]{:S(2)}, u32[]{:S(2)}) collective-permute-start(f32[2,64,128]{2,1,0:T(8,128)} %fusion.9), channel_id=1, source_target_pairs={{0,32},{32,64},{64,96},{96,128},{128,160},{160,192},{192,224},{1,3... | collective-permute-start | bytes 196616 | tf_op jit(solution)/shard_map/ppermute | solution.py:21
  266.7 5.9 %collective-permute-start.26 = (f32[2,64,8]{1,2,0:T(8,128)S(1)}, f32[2,64,8]{1,2,0:T(8,128)S(1)}, u32[]{:S(2)}, u32[]{:S(2)}) collective-permute-start(f32[2,64,8]{1,2,0:T(8,128)S(1)} %pad_maximum_fusion.30), channel_id=1, source_target_pairs={{0,1},{1,2},{2,3},{3,4},{4,5},{5,6},{6,7},{7,8},{8,9},{9,10},{10,1... | collective-permute-start | bytes 12296 | tf_op jit(solution)/shard_map/ppermute | solution.py:21
  272.6 2.1 multiply_subtract_fusion.3
  276.1 5.5 %collective-permute-start.27 = (f32[2,64,128]{2,1,0:T(8,128)}, f32[2,64,128]{2,1,0:T(8,128)}, u32[]{:S(2)}, u32[]{:S(2)}) collective-permute-start(f32[2,64,128]{2,1,0:T(8,128)} %fusion.8), channel_id=1, source_target_pairs={{0,32},{32,64},{64,96},{96,128},{128,160},{160,192},{192,224},{1,3... | collective-permute-start | bytes 196616 | tf_op jit(solution)/shard_map/ppermute | solution.py:21
  308.6 4.8 %collective-permute-start.30 = (f32[2,64,8]{1,2,0:T(8,128)S(1)}, f32[2,64,8]{1,2,0:T(8,128)S(1)}, u32[]{:S(2)}, u32[]{:S(2)}) collective-permute-start(f32[2,64,8]{1,2,0:T(8,128)S(1)} %pad_maximum_fusion.32), channel_id=1, source_target_pairs={{0,1},{1,2},{2,3},{3,4},{4,5},{5,6},{6,7},{7,8},{8,9},{9,10},{10,1... | collective-permute-start | bytes 12296 | tf_op jit(solution)/shard_map/ppermute | solution.py:21
  316.5 6.5 %collective-permute-start.31 = (f32[2,64,128]{2,1,0:T(8,128)S(1)}, f32[2,64,128]{2,1,0:T(8,128)}, u32[]{:S(2)}, u32[]{:S(2)}) collective-permute-start(f32[2,64,128]{2,1,0:T(8,128)S(1)} %bitcast.520), channel_id=1, source_target_pairs={{0,32},{32,64},{64,96},{96,128},{128,160},{160,192},{192,224},{1,3... | collective-permute-start | bytes 196616 | tf_op jit(solution)/shard_map/ppermute | solution.py:21
  323.2 2.0 constant_dynamic-update-slice_fusion.5
  326.3 2.0 constant_dynamic-update-slice_fusion.4
  331.6 2.1 gather_fusion
  334.9 13.8 %all-reduce.33 = (f32[64,128]{1,0:T(8,128)S(1)}, f32[64,64]{1,0:T(8,128)S(1)}) all-reduce(f32[64,128]{1,0:T(8,128)S(1)} %fusion.1, f32[64,64]{1,0:T(8,128)S(1)} %fusion), channel_id=1, replica_groups=mesh['row_0'=4,'row_1'=2,'col_0'=8,'col_1'=2,'col_2'=2] {'row_0'}, use_global_device_ids=true, to_apply=%region_0.1 | all-reduce | flops 12288 | bytes 98304 | tf_op jit(solution)/shard_map/psum | solution.py:26
  348.7 7.6 %all-reduce.36 = (f32[64,128]{1,0:T(8,128)S(1)}, f32[64,64]{1,0:T(8,128)S(1)}) all-reduce(f32[64,128]{1,0:T(8,128)S(1)} %get-tuple-element.18, f32[64,64]{1,0:T(8,128)S(1)} %get-tuple-element.19), channel_id=1, replica_groups=mesh['row_0'=4,'row_1'=2,'col_0'=8,'col_1'=2,'col_2'=2] {'row_1'}, use_global_device_ids=true, to_apply=%region_1.2 | all-reduce | flops 12288 | bytes 98304 | tf_op jit(solution)/shard_map/psum | solution.py:26
  356.3 30.5 %all-reduce.32 = (f32[64,128]{1,0:T(8,128)S(1)}, f32[64,64]{1,0:T(8,128)S(1)}) all-reduce(f32[64,128]{1,0:T(8,128)S(1)} %get-tuple-element.24, f32[64,64]{1,0:T(8,128)S(1)} %get-tuple-element.25), channel_id=1, replica_groups=mesh['row_0'=4,'row_1'=2,'col_0'=8,'col_1'=2,'col_2'=2] {'col_0'}, use_global_device_ids=true, to_apply=%region_2.3 | all-reduce | flops 12288 | bytes 98304 | tf_op jit(solution)/shard_map/psum | solution.py:26
  386.8 13.4 %all-reduce.35 = (f32[64,128]{1,0:T(8,128)S(1)}, f32[64,64]{1,0:T(8,128)S(1)}) all-reduce(f32[64,128]{1,0:T(8,128)S(1)} %get-tuple-element.16, f32[64,64]{1,0:T(8,128)S(1)} %get-tuple-element.17), channel_id=1, replica_groups=mesh['row_0'=4,'row_1'=2,'col_0'=8,'col_1'=2,'col_2'=2] {'col_1'}, use_global_device_ids=true, to_apply=%region_3.4 | all-reduce | flops 12288 | bytes 98304 | tf_op jit(solution)/shard_map/psum | solution.py:26
  400.1 15.4 %all-reduce.34 = (f32[64,128]{1,0:T(8,128)}, f32[64,64]{1,0:T(8,128)}) all-reduce(f32[64,128]{1,0:T(8,128)S(1)} %get-tuple-element.22, f32[64,64]{1,0:T(8,128)S(1)} %get-tuple-element.23), channel_id=1, replica_groups=mesh['row_0'=4,'row_1'=2,'col_0'=8,'col_1'=2,'col_2'=2] {'col_2'}, use_global_device_ids=true, to_apply=%region_4.5 | all-reduce | flops 12288 | bytes 98304 | tf_op jit(solution)/shard_map/psum | solution.py:26
  (543 shorter events, 182.1 us)
Async XLA Ops:
  1.8 26.5 %collective-permute-start = (f32[2,64,128]{2,1,0:T(8,128)S(1)}, f32[2,64,128]{2,1,0:T(8,128)}, u32[]{:S(2)}, u32[]{:S(2)}) collective-permute-start(f32[2,64,128]{2,1,0:T(8,128)S(1)} %bitcast.522), channel_id=1, source_target_pairs={{32,0},{64,32},{96,64},{128,96},{160,128},{192,160},{224,192},{33,... | collective-permute-start | bytes 196616 | tf_op jit(solution)/shard_map/ppermute | solution.py:21
  4.1 12.9 %copy-start.1 = (f32[3,64,8,128]{3,2,1,0:T(8,128)S(1)}, f32[3,64,8,128]{3,2,1,0:T(8,128)}, u32[]{:S(2)}) copy-start(f32[3,64,8,128]{3,2,1,0:T(8,128)} %param.6) | copy-start | bytes 2359300
  4.5 22.6 %collective-permute-start.1 = (f32[2,64,8]{1,2,0:T(8,128)S(1)}, f32[2,64,8]{1,2,0:T(8,128)S(1)}, u32[]{:S(2)}, u32[]{:S(2)}) collective-permute-start(f32[2,64,8]{1,2,0:T(8,128)S(1)} %pad_maximum_fusion.17), channel_id=1, source_target_pairs={{1,0},{2,1},{3,2},{4,3},{5,4},{6,5},{7,6},{8,7},{9,8},{10,9},{11,1... | collective-permute-start | bytes 12296 | tf_op jit(solution)/shard_map/ppermute | solution.py:21
  10.7 14.8 %copy-start.109 = (s32[64]{0:T(128)S(1)}, s32[64]{0:T(128)}, u32[]{:S(2)}) copy-start(s32[64]{0:T(128)} %param.11) | copy-start | bytes 772
  10.7 148.1 %all-to-all-start = ((f32[16,64,128]{2,0,1:T(8,128)}), f32[16,64,128]{2,0,1:T(8,128)}, u32[]{:S(2)}, u32[]{:S(2)}) async-start(f32[16,64,128]{2,0,1:T(8,128)} %copy.1592), calls=%async_computation | async-start | bytes 1048576 | tf_op jit(solution)/shard_map/all_to_all | solution.py:128
  18.0 11.1 %copy-start.57 = (f32[3,64,8,128]{3,2,1,0:T(8,128)S(1)}, f32[3,64,8,128]{3,2,1,0:T(8,128)}, u32[]{:S(2)}) copy-start(f32[3,64,8,128]{3,2,1,0:T(8,128)} %param.7) | copy-start | bytes 2359300
  20.6 10.6 %copy-start.95 = (f32[128]{0:T(128)}, f32[128]{0:T(128)S(1)}, u32[]{:S(2)}) copy-start(f32[128]{0:T(128)S(1)} %get-tuple-element.99) | copy-start | bytes 1540
  21.9 26.0 %copy-start.98 = (f32[128]{0:T(128)}, f32[128]{0:T(128)S(1)}, u32[]{:S(2)}) copy-start(f32[128]{0:T(128)S(1)} %get-tuple-element.88) | copy-start | bytes 1540
  23.8 13.2 %copy-start.101 = (f32[8]{0:T(128)}, f32[8]{0:T(128)S(1)}, u32[]{:S(2)}) copy-start(f32[8]{0:T(128)S(1)} %get-tuple-element.94) | copy-start | bytes 100
  26.4 21.5 %copy-start.68 = (f32[8]{0:T(128)}, f32[8]{0:T(128)S(1)}, u32[]{:S(2)}) copy-start(f32[8]{0:T(128)S(1)} %fusion.20) | copy-start | bytes 100
  33.3 31.9 %copy-start.6 = (f32[64,8,128]{2,1,0:T(8,128)}, f32[64,8,128]{2,1,0:T(8,128)S(1)}, u32[]{:S(2)}) copy-start(f32[64,8,128]{2,1,0:T(8,128)S(1)} %get-tuple-element.98) | copy-start | bytes 786436
  33.6 12.0 %collective-permute-start.2 = (f32[2,64,8]{1,2,0:T(8,128)S(1)}, f32[2,64,8]{1,2,0:T(8,128)S(1)}, u32[]{:S(2)}, u32[]{:S(2)}) collective-permute-start(f32[2,64,8]{1,2,0:T(8,128)S(1)} %pad_maximum_fusion.18), channel_id=1, source_target_pairs={{0,1},{1,2},{2,3},{3,4},{4,5},{5,6},{6,7},{7,8},{8,9},{9,10},{10,1... | collective-permute-start | bytes 12296 | tf_op jit(solution)/shard_map/ppermute | solution.py:21
  39.9 8.0 %collective-permute-start.3 = (f32[2,64,128]{2,1,0:T(8,128)S(1)}, f32[2,64,128]{2,1,0:T(8,128)S(1)}, u32[]{:S(2)}, u32[]{:S(2)}) collective-permute-start(f32[2,64,128]{2,1,0:T(8,128)S(1)} %bitcast.519), channel_id=1, source_target_pairs={{0,32},{32,64},{64,96},{96,128},{128,160},{160,192},{192,224},{1,3... | collective-permute-start | bytes 196616 | tf_op jit(solution)/shard_map/ppermute | solution.py:21
  50.2 7.0 %collective-permute-start.5 = (f32[2,64,8]{1,2,0:T(8,128)S(1)}, f32[2,64,8]{1,2,0:T(8,128)S(1)}, u32[]{:S(2)}, u32[]{:S(2)}) collective-permute-start(f32[2,64,8]{1,2,0:T(8,128)S(1)} %pad_maximum_fusion.19), channel_id=1, source_target_pairs={{1,0},{2,1},{3,2},{4,3},{5,4},{6,5},{7,6},{8,7},{9,8},{10,9},{11,1... | collective-permute-start | bytes 12296 | tf_op jit(solution)/shard_map/ppermute | solution.py:21
  55.9 6.7 %collective-permute-start.4 = (f32[2,64,128]{2,1,0:T(8,128)}, f32[2,64,128]{2,1,0:T(8,128)S(1)}, u32[]{:S(2)}, u32[]{:S(2)}) collective-permute-start(f32[2,64,128]{2,1,0:T(8,128)} %fusion.16), channel_id=1, source_target_pairs={{32,0},{64,32},{96,64},{128,96},{160,128},{192,160},{224,192},{33,... | collective-permute-start | bytes 196616 | tf_op jit(solution)/shard_map/ppermute | solution.py:21
  67.6 12.6 %copy-start.76 = (f32[128]{0:T(128)S(1)}, f32[128]{0:T(128)}, u32[]{:S(2)}) copy-start(f32[128]{0:T(128)} %copy-done.75) | copy-start | bytes 1540
  67.6 12.6 %copy-start.99 = (f32[128]{0:T(128)S(1)}, f32[128]{0:T(128)}, u32[]{:S(2)}) copy-start(f32[128]{0:T(128)} %copy-done.98) | copy-start | bytes 1540
  67.9 12.2 %collective-permute-start.6 = (f32[2,64,8]{1,2,0:T(8,128)S(1)}, f32[2,64,8]{1,2,0:T(8,128)S(1)}, u32[]{:S(2)}, u32[]{:S(2)}) collective-permute-start(f32[2,64,8]{1,2,0:T(8,128)S(1)} %pad_maximum_fusion.20), channel_id=1, source_target_pairs={{0,1},{1,2},{2,3},{3,4},{4,5},{5,6},{6,7},{7,8},{8,9},{9,10},{10,1... | collective-permute-start | bytes 12296 | tf_op jit(solution)/shard_map/ppermute | solution.py:21
  74.1 10.2 %collective-permute-start.7 = (f32[2,64,128]{2,1,0:T(8,128)}, f32[2,64,128]{2,1,0:T(8,128)}, u32[]{:S(2)}, u32[]{:S(2)}) collective-permute-start(f32[2,64,128]{2,1,0:T(8,128)} %fusion.15), channel_id=1, source_target_pairs={{0,32},{32,64},{64,96},{96,128},{128,160},{160,192},{192,224},{1,3... | collective-permute-start | bytes 196616 | tf_op jit(solution)/shard_map/ppermute | solution.py:21
  88.0 6.9 %collective-permute-start.9 = (f32[2,64,8]{1,2,0:T(8,128)S(1)}, f32[2,64,8]{1,2,0:T(8,128)S(1)}, u32[]{:S(2)}, u32[]{:S(2)}) collective-permute-start(f32[2,64,8]{1,2,0:T(8,128)S(1)} %pad_maximum_fusion.21), channel_id=1, source_target_pairs={{1,0},{2,1},{3,2},{4,3},{5,4},{6,5},{7,6},{8,7},{9,8},{10,9},{11,1... | collective-permute-start | bytes 12296 | tf_op jit(solution)/shard_map/ppermute | solution.py:21
  93.6 6.8 %collective-permute-start.8 = (f32[2,64,128]{2,1,0:T(8,128)}, f32[2,64,128]{2,1,0:T(8,128)}, u32[]{:S(2)}, u32[]{:S(2)}) collective-permute-start(f32[2,64,128]{2,1,0:T(8,128)} %fusion.14), channel_id=1, source_target_pairs={{32,0},{64,32},{96,64},{128,96},{160,128},{192,160},{224,192},{33,... | collective-permute-start | bytes 196616 | tf_op jit(solution)/shard_map/ppermute | solution.py:21
  104.5 13.6 %collective-permute-start.10 = (f32[2,64,8]{1,2,0:T(8,128)S(1)}, f32[2,64,8]{1,2,0:T(8,128)S(1)}, u32[]{:S(2)}, u32[]{:S(2)}) collective-permute-start(f32[2,64,8]{1,2,0:T(8,128)S(1)} %pad_maximum_fusion.22), channel_id=1, source_target_pairs={{0,1},{1,2},{2,3},{3,4},{4,5},{5,6},{6,7},{7,8},{8,9},{9,10},{10,1... | collective-permute-start | bytes 12296 | tf_op jit(solution)/shard_map/ppermute | solution.py:21
  113.2 9.7 %collective-permute-start.11 = (f32[2,64,128]{2,1,0:T(8,128)}, f32[2,64,128]{2,1,0:T(8,128)}, u32[]{:S(2)}, u32[]{:S(2)}) collective-permute-start(f32[2,64,128]{2,1,0:T(8,128)} %bitcast.74), channel_id=1, source_target_pairs={{0,32},{32,64},{64,96},{96,128},{128,160},{160,192},{192,224},{1,3... | collective-permute-start | bytes 196616 | tf_op jit(solution)/shard_map/ppermute | solution.py:21
  125.2 42.0 %copy-start.13 = (f32[64,8,128]{2,1,0:T(8,128)}, f32[64,8,128]{2,1,0:T(8,128)S(1)}, u32[]{:S(2)}) copy-start(f32[64,8,128]{2,1,0:T(8,128)S(1)} %get-tuple-element.65) | copy-start | bytes 786436
  127.8 7.9 %collective-permute-start.13 = (f32[2,64,8]{1,2,0:T(8,128)S(1)}, f32[2,64,8]{1,2,0:T(8,128)S(1)}, u32[]{:S(2)}, u32[]{:S(2)}) collective-permute-start(f32[2,64,8]{1,2,0:T(8,128)S(1)} %pad_maximum_fusion.23), channel_id=1, source_target_pairs={{1,0},{2,1},{3,2},{4,3},{5,4},{6,5},{7,6},{8,7},{9,8},{10,9},{11,1... | collective-permute-start | bytes 12296 | tf_op jit(solution)/shard_map/ppermute | solution.py:21
  134.2 7.2 %collective-permute-start.12 = (f32[2,64,128]{2,1,0:T(8,128)}, f32[2,64,128]{2,1,0:T(8,128)}, u32[]{:S(2)}, u32[]{:S(2)}) collective-permute-start(f32[2,64,128]{2,1,0:T(8,128)} %fusion.13), channel_id=1, source_target_pairs={{32,0},{64,32},{96,64},{128,96},{160,128},{192,160},{224,192},{33,... | collective-permute-start | bytes 196616 | tf_op jit(solution)/shard_map/ppermute | solution.py:21
  145.5 15.3 %collective-permute-start.14 = (f32[2,64,8]{1,2,0:T(8,128)S(1)}, f32[2,64,8]{1,2,0:T(8,128)S(1)}, u32[]{:S(2)}, u32[]{:S(2)}) collective-permute-start(f32[2,64,8]{1,2,0:T(8,128)S(1)} %pad_maximum_fusion.24), channel_id=1, source_target_pairs={{0,1},{1,2},{2,3},{3,4},{4,5},{5,6},{6,7},{7,8},{8,9},{9,10},{10,1... | collective-permute-start | bytes 12296 | tf_op jit(solution)/shard_map/ppermute | solution.py:21
  151.8 9.9 %copy-start.38 = (f32[64,8,1]{2,1,0:T(8,128)S(1)}, f32[64,8,1]{2,1,0:T(8,128)}, u32[]{:S(2)}) copy-start(f32[64,8,1]{2,1,0:T(8,128)} %copy-done.37) | copy-start | bytes 6148
  151.8 9.9 %copy-start.77 = (f32[128]{0:T(128)S(1)}, f32[128]{0:T(128)}, u32[]{:S(2)}) copy-start(f32[128]{0:T(128)} %copy-done.75) | copy-start | bytes 1540
  153.2 13.2 %collective-permute-start.15 = (f32[2,64,128]{2,1,0:T(8,128)}, f32[2,64,128]{2,1,0:T(8,128)}, u32[]{:S(2)}, u32[]{:S(2)}) collective-permute-start(f32[2,64,128]{2,1,0:T(8,128)} %fusion.12), channel_id=1, source_target_pairs={{0,32},{32,64},{64,96},{96,128},{128,160},{160,192},{192,224},{1,3... | collective-permute-start | bytes 196616 | tf_op jit(solution)/shard_map/ppermute | solution.py:21
  169.6 5.6 %collective-permute-start.17 = (f32[2,64,8]{1,2,0:T(8,128)S(1)}, f32[2,64,8]{1,2,0:T(8,128)S(1)}, u32[]{:S(2)}, u32[]{:S(2)}) collective-permute-start(f32[2,64,8]{1,2,0:T(8,128)S(1)} %pad_maximum_fusion.25), channel_id=1, source_target_pairs={{1,0},{2,1},{3,2},{4,3},{5,4},{6,5},{7,6},{8,7},{9,8},{10,9},{11,1... | collective-permute-start | bytes 12296 | tf_op jit(solution)/shard_map/ppermute | solution.py:21
  173.9 6.9 %collective-permute-start.16 = (f32[2,64,128]{2,1,0:T(8,128)}, f32[2,64,128]{2,1,0:T(8,128)}, u32[]{:S(2)}, u32[]{:S(2)}) collective-permute-start(f32[2,64,128]{2,1,0:T(8,128)} %fusion.11), channel_id=1, source_target_pairs={{32,0},{64,32},{96,64},{128,96},{160,128},{192,160},{224,192},{33,... | collective-permute-start | bytes 196616 | tf_op jit(solution)/shard_map/ppermute | solution.py:21
  185.0 12.6 %collective-permute-start.18 = (f32[2,64,8]{1,2,0:T(8,128)S(1)}, f32[2,64,8]{1,2,0:T(8,128)S(1)}, u32[]{:S(2)}, u32[]{:S(2)}) collective-permute-start(f32[2,64,8]{1,2,0:T(8,128)S(1)} %pad_maximum_fusion.26), channel_id=1, source_target_pairs={{0,1},{1,2},{2,3},{3,4},{4,5},{5,6},{6,7},{7,8},{8,9},{9,10},{10,1... | collective-permute-start | bytes 12296 | tf_op jit(solution)/shard_map/ppermute | solution.py:21
  193.2 10.3 %collective-permute-start.19 = (f32[2,64,128]{2,1,0:T(8,128)S(1)}, f32[2,64,128]{2,1,0:T(8,128)}, u32[]{:S(2)}, u32[]{:S(2)}) collective-permute-start(f32[2,64,128]{2,1,0:T(8,128)S(1)} %bitcast.521), channel_id=1, source_target_pairs={{0,32},{32,64},{64,96},{96,128},{128,160},{160,192},{192,224},{1,3... | collective-permute-start | bytes 196616 | tf_op jit(solution)/shard_map/ppermute | solution.py:21
  209.1 7.7 %collective-permute-start.21 = (f32[2,64,8]{1,2,0:T(8,128)S(1)}, f32[2,64,8]{1,2,0:T(8,128)S(1)}, u32[]{:S(2)}, u32[]{:S(2)}) collective-permute-start(f32[2,64,8]{1,2,0:T(8,128)S(1)} %pad_maximum_fusion.27), channel_id=1, source_target_pairs={{1,0},{2,1},{3,2},{4,3},{5,4},{6,5},{7,6},{8,7},{9,8},{10,9},{11,1... | collective-permute-start | bytes 12296 | tf_op jit(solution)/shard_map/ppermute | solution.py:21
  215.5 6.8 %collective-permute-start.20 = (f32[2,64,128]{2,1,0:T(8,128)}, f32[2,64,128]{2,1,0:T(8,128)}, u32[]{:S(2)}, u32[]{:S(2)}) collective-permute-start(f32[2,64,128]{2,1,0:T(8,128)} %fusion.10), channel_id=1, source_target_pairs={{32,0},{64,32},{96,64},{128,96},{160,128},{192,160},{224,192},{33,... | collective-permute-start | bytes 196616 | tf_op jit(solution)/shard_map/ppermute | solution.py:21
  227.2 13.3 %collective-permute-start.22 = (f32[2,64,8]{1,2,0:T(8,128)S(1)}, f32[2,64,8]{1,2,0:T(8,128)S(1)}, u32[]{:S(2)}, u32[]{:S(2)}) collective-permute-start(f32[2,64,8]{1,2,0:T(8,128)S(1)} %pad_maximum_fusion.28), channel_id=1, source_target_pairs={{0,1},{1,2},{2,3},{3,4},{4,5},{5,6},{6,7},{7,8},{8,9},{9,10},{10,1... | collective-permute-start | bytes 12296 | tf_op jit(solution)/shard_map/ppermute | solution.py:21
  234.6 10.4 %collective-permute-start.23 = (f32[2,64,128]{2,1,0:T(8,128)}, f32[2,64,128]{2,1,0:T(8,128)}, u32[]{:S(2)}, u32[]{:S(2)}) collective-permute-start(f32[2,64,128]{2,1,0:T(8,128)} %fusion.9), channel_id=1, source_target_pairs={{0,32},{32,64},{64,96},{96,128},{128,160},{160,192},{192,224},{1,3... | collective-permute-start | bytes 196616 | tf_op jit(solution)/shard_map/ppermute | solution.py:21
  248.5 8.0 %collective-permute-start.25 = (f32[2,64,8]{1,2,0:T(8,128)S(1)}, f32[2,64,8]{1,2,0:T(8,128)S(1)}, u32[]{:S(2)}, u32[]{:S(2)}) collective-permute-start(f32[2,64,8]{1,2,0:T(8,128)S(1)} %pad_maximum_fusion.29), channel_id=1, source_target_pairs={{1,0},{2,1},{3,2},{4,3},{5,4},{6,5},{7,6},{8,7},{9,8},{10,9},{11,1... | collective-permute-start | bytes 12296 | tf_op jit(solution)/shard_map/ppermute | solution.py:21
  255.2 6.8 %collective-permute-start.24 = (f32[2,64,128]{2,1,0:T(8,128)}, f32[2,64,128]{2,1,0:T(8,128)}, u32[]{:S(2)}, u32[]{:S(2)}) collective-permute-start(f32[2,64,128]{2,1,0:T(8,128)} %bitcast.148), channel_id=1, source_target_pairs={{32,0},{64,32},{96,64},{128,96},{160,128},{192,160},{224,192},{33,... | collective-permute-start | bytes 196616 | tf_op jit(solution)/shard_map/ppermute | solution.py:21
  266.7 15.0 %collective-permute-start.26 = (f32[2,64,8]{1,2,0:T(8,128)S(1)}, f32[2,64,8]{1,2,0:T(8,128)S(1)}, u32[]{:S(2)}, u32[]{:S(2)}) collective-permute-start(f32[2,64,8]{1,2,0:T(8,128)S(1)} %pad_maximum_fusion.30), channel_id=1, source_target_pairs={{0,1},{1,2},{2,3},{3,4},{4,5},{5,6},{6,7},{7,8},{8,9},{9,10},{10,1... | collective-permute-start | bytes 12296 | tf_op jit(solution)/shard_map/ppermute | solution.py:21
  276.1 10.9 %collective-permute-start.27 = (f32[2,64,128]{2,1,0:T(8,128)}, f32[2,64,128]{2,1,0:T(8,128)}, u32[]{:S(2)}, u32[]{:S(2)}) collective-permute-start(f32[2,64,128]{2,1,0:T(8,128)} %fusion.8), channel_id=1, source_target_pairs={{0,32},{32,64},{64,96},{96,128},{128,160},{160,192},{192,224},{1,3... | collective-permute-start | bytes 196616 | tf_op jit(solution)/shard_map/ppermute | solution.py:21
  291.8 7.7 %collective-permute-start.29 = (f32[2,64,8]{1,2,0:T(8,128)S(1)}, f32[2,64,8]{1,2,0:T(8,128)S(1)}, u32[]{:S(2)}, u32[]{:S(2)}) collective-permute-start(f32[2,64,8]{1,2,0:T(8,128)S(1)} %pad_maximum_fusion.31), channel_id=1, source_target_pairs={{1,0},{2,1},{3,2},{4,3},{5,4},{6,5},{7,6},{8,7},{9,8},{10,9},{11,1... | collective-permute-start | bytes 12296 | tf_op jit(solution)/shard_map/ppermute | solution.py:21
  298.2 6.8 %collective-permute-start.28 = (f32[2,64,128]{2,1,0:T(8,128)}, f32[2,64,128]{2,1,0:T(8,128)}, u32[]{:S(2)}, u32[]{:S(2)}) collective-permute-start(f32[2,64,128]{2,1,0:T(8,128)} %fusion.7), channel_id=1, source_target_pairs={{32,0},{64,32},{96,64},{128,96},{160,128},{192,160},{224,192},{33,... | collective-permute-start | bytes 196616 | tf_op jit(solution)/shard_map/ppermute | solution.py:21
  308.6 14.3 %collective-permute-start.30 = (f32[2,64,8]{1,2,0:T(8,128)S(1)}, f32[2,64,8]{1,2,0:T(8,128)S(1)}, u32[]{:S(2)}, u32[]{:S(2)}) collective-permute-start(f32[2,64,8]{1,2,0:T(8,128)S(1)} %pad_maximum_fusion.32), channel_id=1, source_target_pairs={{0,1},{1,2},{2,3},{3,4},{4,5},{5,6},{6,7},{7,8},{8,9},{9,10},{10,1... | collective-permute-start | bytes 12296 | tf_op jit(solution)/shard_map/ppermute | solution.py:21
  316.5 8.9 %collective-permute-start.31 = (f32[2,64,128]{2,1,0:T(8,128)S(1)}, f32[2,64,128]{2,1,0:T(8,128)}, u32[]{:S(2)}, u32[]{:S(2)}) collective-permute-start(f32[2,64,128]{2,1,0:T(8,128)S(1)} %bitcast.520), channel_id=1, source_target_pairs={{0,32},{32,64},{64,96},{96,128},{128,160},{160,192},{192,224},{1,3... | collective-permute-start | bytes 196616 | tf_op jit(solution)/shard_map/ppermute | solution.py:21
  330.8 84.7 %copy-start.58 = (f32[1,64,8,128]{3,2,1,0:T(8,128)S(1)}, f32[1,64,8,128]{3,2,1,0:T(8,128)}, u32[]{:S(2)}) copy-start(f32[1,64,8,128]{3,2,1,0:T(8,128)} %get-tuple-element.31) | copy-start | bytes 786436
  330.8 84.7 %copy-start.59 = (f32[1,64,8,128]{3,2,1,0:T(8,128)S(1)}, f32[1,64,8,128]{3,2,1,0:T(8,128)}, u32[]{:S(2)}) copy-start(f32[1,64,8,128]{3,2,1,0:T(8,128)} %get-tuple-element.29) | copy-start | bytes 786436
  (95 other events, 484.7 us)
where the time goes:
time: 420 us; the launch traced here: 416 us
  starting transfers between devices  119 us (28%)
  local copies, waits for them, and re-layouts  106 us (25%)
  other arithmetic  98.7 us (24%)
  blocking collectives  80.6 us (19%)
  waiting for transfers between devices  7.37 us (2%)
    ppermute x32, starting transfers between devices, from_behind(): return lax.ppermute(block, axis, route)  112 us
    psum x5, blocking collectives, by_axis(): array = lax.psum(array, axis)  80.6 us
    slice x45, local copies, waits for them, and re-layouts, forward(): lax.slice_in_dim(field, 1, count, axis=axis)  33.4 us
    sub x8, other arithmetic, magnetic(): h_z = h_z - time_step * (ey_dx + psi_hzx - ex_dy - psi_hzy)  15.1 us
    sub x8, other arithmetic, magnetic(): h_x = h_x - time_step * (ez_dy + psi_hxy - ey_dz)  14.7 us
    another operation x24, local copies, waits for them, and re-layouts, forward(): jnp.expand_dims(plane, axis)  12.5 us
    sub x7, other arithmetic, magnetic(): h_y = h_y - time_step * (ex_dz - ez_dx - psi_hyx)  12 us
    add x6, other arithmetic, electric(): e_z = e_z + e_coef * (hy_dx + psi_ezx - hx_dy - psi_ezy)  10.3 us
  transfers between devices with their start and end apart: 33, of which 5 were waited for; matrix products, arithmetic and copies ran while one was open for 38% of the time, Pallas kernels for 0%

commit v1 on v0

v1 whole, which is shorter than its diff:
```python
import functools

import jax
import jax.numpy as jnp
from jax import lax
from jax.experimental import pallas as pl
from jax.experimental.pallas import tpu as pltpu
from jax.sharding import PartitionSpec as P

STEPS = 8
time_step = 0.5
sigma_top = 4.0
alpha_shift = 0.05
MESH = pl.DeviceIdType.MESH
TILE = (8, 128)
f32 = jnp.float32


def absorber(positions, total, low, high):
    depth = jnp.maximum(
        jnp.maximum((low - positions) / low, (positions - (total - 1.0 - high)) / high), 0.0
    )
    sigma = sigma_top * (depth * depth * depth)
    damp = jnp.exp(-(sigma + alpha_shift) * time_step)
    gain = sigma / (sigma + alpha_shift) * (damp - 1.0)
    return damp, gain


def kernel(
    n_row, n_col, nz, unroll,
    e_in, h_in, c_in, basis, pml, snap,
    e_out, h_out, coef_out, gram_out,
    F, CE, PSI, K,
    sxd, sxu, syd, syu, scb,
    rxd, rxu, ryd, ryu, rca, rcb,
    W, R, RA, PB, G,
    in_sem, out_sem, hs_sem, hr_sem, bs_sem, br_sem, own_sem,
    as_sem, ar_sem, ps_sem, pr_sem, gs_sem, gr_sem,
):
    row = lax.axis_index("row")
    col = lax.axis_index("col")
    n_a, n_b = n_row * 2, n_col // 2
    y_lo = lax.rem(lax.div(col, 2), 2)
    a_me = row * 2 + y_lo
    b_me = lax.div(col, 4) * 2 + lax.rem(col, 2)

    def a_device(m):
        return (lax.div(m, 2), lax.div(col, 4) * 4 + lax.rem(m, 2) * 2 + lax.rem(col, 2))

    def b_device(m):
        return (row, lax.div(m, 2) * 4 + y_lo * 2 + lax.rem(m, 2))

    loads = [
        pltpu.make_async_copy(e_in, F.at[0:3], in_sem.at[0]),
        pltpu.make_async_copy(h_in, F.at[3:6], in_sem.at[1]),
        pltpu.make_async_copy(c_in, CE, in_sem.at[2]),
    ]
    for copy in loads:
        copy.start()
    modes_here = basis.shape[0]

    def own_modes():
        return pltpu.make_async_copy(
            basis.at[:, pl.ds(pl.multiple_of(row * 8, 8), 8), :],
            W.at[pl.ds(row * modes_here, modes_here)],
            own_sem.at[0],
        )

    own_modes().start()

    barrier = pltpu.get_barrier_semaphore()

    def greet(device):
        pl.semaphore_signal(barrier, inc=1, device_id=device, device_id_type=MESH)

    @pl.loop(1, n_a)
    def _(j):
        greet(a_device(lax.rem(a_me + j, n_a)))

    @pl.loop(1, n_b)
    def _(j):
        greet(b_device(lax.rem(b_me + j, n_b)))

    up_x, dn_x = row < n_row - 1, row > 0
    up_y, dn_y = col < n_col - 1, col > 0
    ca_out, ca_in = up_x & dn_y, dn_x & up_y

    @pl.when(up_y)
    def _():
        greet((row, col + 1))

    @pl.when(dn_y)
    def _():
        greet((row, col - 1))

    @pl.when(ca_out)
    def _():
        greet((row + 1, col - 1))

    @pl.when(ca_in)
    def _():
        greet((row - 1, col + 1))

    greeted = n_a - 1 + n_b - 1
    for flag in (up_y, dn_y, ca_out, ca_in):
        greeted = greeted + flag.astype(jnp.int32)

    sub = lax.broadcasted_iota(jnp.int32, TILE, 0)
    lane = lax.broadcasted_iota(jnp.int32, TILE, 1)
    w = [jnp.full(TILE, pml[i], jnp.int32).astype(f32) for i in range(4)]
    x_pos = (row * 8 + sub).astype(f32)
    y_pos = (col * 128 + lane).astype(f32)
    full_x, full_y = float(n_row * 8), float(n_col * 128)
    hdx, hgx = absorber(x_pos + 0.5, full_x, w[0], w[1])
    hdy, hgy = absorber(y_pos + 0.5, full_y, w[2], w[3])
    edx, egx = absorber(x_pos, full_x, w[0], w[1])
    edy, egy = absorber(y_pos, full_y, w[2], w[3])
    _, gxm = absorber((row * 8 - 1 + 0 * sub).astype(f32) + 0.5, full_x, w[0], w[1])
    _, gym = absorber((col * 128 - 1 + 0 * lane).astype(f32) + 0.5, full_y, w[2], w[3])
    s7, s0, l127, l0 = sub == 7, sub == 0, lane == 127, lane == 0
    zero = jnp.zeros(TILE, f32)
    coeffs = [
        hdx, hgx, hdy, hgy, edx, egx, edy, egy,
        jnp.where(s7, 0.5 * (1.0 + hgx), zero), jnp.where(s7, hgx, zero),
        jnp.where(l127, 0.5 * (1.0 + hgy), zero), jnp.where(l127, hgy, zero),
        0.5 * (1.0 + gxm) * dn_x.astype(f32), 0.5 * (1.0 + gym) * dn_y.astype(f32),
    ]
    for i, value in enumerate(coeffs):
        K[i] = value
    HDX, HGX, HDY, HGY, EDX, EGX, EDY, EGY, CXU, PXU, CYU, PYU, CXD, CYD = range(14)

    @pl.loop(0, nz)
    def _(z):
        for i in range(8):
            PSI[i, z] = zero

    def clear(ref, wanted):
        @pl.when(wanted)
        def _():
            @pl.loop(0, STEPS)
            def _(n):
                ref[n] = jnp.zeros(ref.shape[1:], f32)

    clear(rxd, ~up_x)
    clear(rxu, ~dn_x)
    clear(ryd, ~up_y)
    clear(ryu, ~dn_y)
    clear(rca, ~ca_in)
    clear(rcb, ~ca_out)

    def row_of(ref, n, c, z):
        return jnp.broadcast_to(ref[n, c, pl.ds(z, 1), :], TILE)

    def roll_l(v, by):
        return pltpu.roll(v, by, 1)

    def roll_s(v, by):
        return pltpu.roll(v, by, 0)

    def partial_h(E, H, psi, ex_next, ey_next):
        ex, ey, ez = E
        hx, hy, hz = H
        ez_dy = jnp.where(l127, 0.0, roll_l(ez, 127)) - ez
        ex_dy = jnp.where(l127, 0.0, roll_l(ex, 127)) - ex
        ez_dx = jnp.where(s7, 0.0, roll_s(ez, 7)) - ez
        ey_dx = jnp.where(s7, 0.0, roll_s(ey, 7)) - ey
        ey_dz = ey_next - ey
        ex_dz = ex_next - ex
        p0 = K[HDY] * psi[0] + K[HGY] * ez_dy
        p1 = K[HDX] * psi[1] + K[HGX] * ez_dx
        p2 = K[HDX] * psi[2] + K[HGX] * ey_dx
        p3 = K[HDY] * psi[3] + K[HGY] * ex_dy
        hx = hx - time_step * (ez_dy + p0 - ey_dz)
        hy = hy - time_step * (ex_dz - ez_dx - p1)
        hz = hz - time_step * (ey_dx + p2 - ex_dy - p3)
        return (hx, hy, hz), (p0, p1, p2, p3)

    def pack_e(n, z, E, pd, pb):
        ex, ey, ez = E
        sxd[n, 0, pl.ds(z, 1), :] = ey[0:1, :]
        sxd[n, 1, pl.ds(z, 1), :] = ez[0:1, :]
        low, high = lane == z, lane == 64 + z
        pd = jnp.where(low, roll_l(ex, z), jnp.where(high, roll_l(ez, 64 + z), pd))
        pb = jnp.where(high, roll_l(ey, lax.rem(65 + z, 128)), pb)
        return pd, pb

    def finish_h(n, z, E, H, psi, ex_next, ey_next, pu):
        H, psi = partial_h(E, H, psi, ex_next, ey_next)
        for i in range(3):
            F[3 + i, z] = H[i]
        for i in range(4):
            PSI[i, z] = psi[i]
        sxu[n, 0, pl.ds(z, 1), :] = H[1][7:8, :]
        sxu[n, 1, pl.ds(z, 1), :] = H[2][7:8, :]
        low, high = lane == z, lane == 64 + z
        return jnp.where(
            low, roll_l(H[0], z + 1), jnp.where(high, roll_l(H[2], lax.rem(65 + z, 128)), pu)
        )

    def electric(n, z, yd, yu, ca, hx_prev, hy_prev):
        ex, ey, ez = F[0, z], F[1, z], F[2, z]
        hx, hy, hz = F[3, z], F[4, z], F[5, z]
        p0, p1, p2, p3 = PSI[0, z], PSI[1, z], PSI[2, z], PSI[3, z]
        ey8, ez8 = row_of(rxd, n, 0, z), row_of(rxd, n, 1, z)
        ex128, ez128 = roll_l(yd, 127 - z), roll_l(yd, 63 - z)
        hy = hy + K[CXU] * ez8
        p1 = p1 + K[PXU] * ez8
        hx = hx - K[CYU] * ez128
        p0 = p0 + K[PYU] * ez128
        hz = hz - K[CXU] * ey8 + K[CYU] * ex128
        p2 = p2 + K[PXU] * ey8
        p3 = p3 + K[PYU] * ex128
        hy_m = row_of(rxu, n, 0, z) + K[CXD] * ez
        hz_m = row_of(rxu, n, 1, z) - K[CXD] * ey + K[CYU] * roll_l(ca, 127 - z)
        hx_w = roll_l(yu, lax.rem(128 - z, 128)) - K[CYD] * ez
        hz_w = roll_l(yu, 64 - z) + K[CYD] * ex
        hz_dy = hz - jnp.where(l0, hz_w, roll_l(hz, 1))
        hx_dy = hx - jnp.where(l0, hx_w, roll_l(hx, 1))
        hz_dx = hz - jnp.where(s0, hz_m, roll_s(hz, 1))
        hy_dx = hy - jnp.where(s0, hy_m, roll_s(hy, 1))
        hy_dz = hy - hy_prev
        hx_dz = hx - hx_prev
        q0 = K[EDY] * PSI[4, z] + K[EGY] * hz_dy
        q1 = K[EDX] * PSI[5, z] + K[EGX] * hz_dx
        q2 = K[EDX] * PSI[6, z] + K[EGX] * hy_dx
        q3 = K[EDY] * PSI[7, z] + K[EGY] * hx_dy
        PSI[4, z], PSI[5, z], PSI[6, z], PSI[7, z] = q0, q1, q2, q3
        ce = CE[z]
        ex = ex + ce * (hz_dy + q0 - hy_dz)
        ey = ey + ce * (hx_dz - hz_dx - q1)
        ez = ez + ce * (hy_dx + q2 - hx_dy - q3)
        F[0, z], F[1, z], F[2, z] = ex, ey, ez
        return (ex, ey, ez), (hx, hy, hz), (p0, p1, p2, p3)

    def messages(n):
        def send(flag, i, src, dst, device):
            copy = pltpu.make_async_remote_copy(
                src_ref=src.at[n], dst_ref=dst.at[n],
                send_sem=hs_sem.at[n, i], recv_sem=hr_sem.at[n, i],
                device_id=device, device_id_type=MESH,
            )
            return flag, copy

        sends = [
            send(dn_x, 0, sxd, rxd, (row - 1, col)),
            send(up_x, 1, sxu, rxu, (row + 1, col)),
            send(dn_y, 2, syd, ryd, (row, col - 1)),
            send(up_y, 3, syu, ryu, (row, col + 1)),
            send(ca_out, 4, syd, rca, (row + 1, col - 1)),
            send(ca_in, 5, scb, rcb, (row - 1, col + 1)),
        ]
        arrives = [up_x, dn_x, up_y, dn_y, ca_in, ca_out]
        return sends, arrives

    def start_sends(n):
        for flag, copy in messages(n)[0]:
            pl.when(flag)(copy.start)

    def wait_arrivals(n):
        sends, arrives = messages(n)
        for (_, copy), flag in zip(sends, arrives):
            pl.when(flag)(copy.wait_recv)

    def wait_sends(n):
        for flag, copy in messages(n)[0]:
            pl.when(flag)(copy.wait_send)

    def mode_copy(j):
        dest = lax.rem(row + j, n_row)
        return pltpu.make_async_remote_copy(
            src_ref=basis.at[:, pl.ds(pl.multiple_of(dest * 8, 8), 8), :],
            dst_ref=W.at[pl.ds(row * modes_here, modes_here)],
            send_sem=bs_sem.at[j], recv_sem=br_sem.at[j],
            device_id=(dest, col), device_id_type=MESH,
        )

    def looped(first, last, step, carry):
        return lax.fori_loop(
            0, (last - first) // unroll,
            lambda i, c: functools.reduce(
                lambda c, u: step(first + i * unroll + u, c), range(unroll), c
            ),
            carry,
        )

    for copy in loads:
        copy.wait()

    def fields(base, z):
        return F[base, z], F[base + 1, z], F[base + 2, z]

    psi_zero = (zero,) * 4

    def opening(z, carry):
        E, (pd, pb, pu) = carry
        ahead = fields(0, z)
        pd, pb = pack_e(0, z, ahead, pd, pb)
        pu = finish_h(0, z - 1, E, fields(3, z - 1), psi_zero, ahead[0], ahead[1], pu)
        return ahead, (pd, pb, pu)

    first = fields(0, 0)
    pd, pb = pack_e(0, 0, first, zero, zero)
    last, (pd, pb, pu) = looped(1, nz, opening, (first, (pd, pb, zero)))
    pu = finish_h(0, nz - 1, last, fields(3, nz - 1), psi_zero, zero, zero, pu)
    syd[0], scb[0], syu[0] = pd, pb, pu
    pl.semaphore_wait(barrier, greeted)
    start_sends(0)

    def arrived(n):
        wait_arrivals(n)
        ca = jnp.broadcast_to(rca[n, 7:8, :], TILE)
        yu = ryu[n] - K[CXU] * jnp.broadcast_to(rcb[n, 0:1, :], TILE)
        return ryd[n], yu, ca

    @pl.loop(0, STEPS - 1)
    def _(n):
        @pl.when(n < n_row - 1)
        def _():
            mode_copy(n + 1).start()

        yd, yu, ca = arrived(n)

        def body(z, carry):
            E, H, psi, (pd, pb, pu) = carry
            E2, H2, psi2 = electric(n, z, yd, yu, ca, H[0], H[1])
            pd, pb = pack_e(n + 1, z, E2, pd, pb)
            pu = finish_h(n + 1, z - 1, E, H, psi, E2[0], E2[1], pu)
            return E2, H2, psi2, (pd, pb, pu)

        E, H, psi = electric(n, 0, yd, yu, ca, zero, zero)
        pd, pb = pack_e(n + 1, 0, E, zero, zero)
        E, H, psi, (pd, pb, pu) = looped(1, nz, body, (E, H, psi, (pd, pb, zero)))
        pu = finish_h(n + 1, nz - 1, E, H, psi, zero, zero, pu)
        syd[n + 1], scb[n + 1], syu[n + 1] = pd, pb, pu
        start_sends(n + 1)

    yd, yu, ca = arrived(STEPS - 1)

    def closing(z, carry):
        _, H, _ = electric(STEPS - 1, z, yd, yu, ca, carry[0], carry[1])
        F[3, z], F[4, z], F[5, z] = H
        return H[0], H[1]

    carry = closing(0, (zero, zero))
    looped(1, nz, closing, carry)

    stores = [
        pltpu.make_async_copy(F.at[0:3], e_out, out_sem.at[0]),
        pltpu.make_async_copy(F.at[3:6], h_out, out_sem.at[1]),
    ]
    for copy in stores:
        copy.start()

    count = snap.shape[0]
    rank = modes_here * n_row

    @pl.loop(0, count)
    def _(s):
        plane = snap[s]
        W[rank + s] = F[lax.div(plane, nz), lax.rem(plane, nz)]

    own_modes().wait()

    @pl.loop(1, n_row)
    def _(j):
        mode_copy(j).wait_recv()

    both = jnp.zeros((count, rank + count), f32)
    for x in range(8):
        both = both + lax.dot_general(
            W[rank:rank + count, x, :], W[:, x, :], (((1,), (1,)), ((), ())),
            precision=lax.Precision.HIGHEST, preferred_element_type=f32,
        )
    R[0:8] = both[:, :rank].reshape(8, 8, 128)
    gram = both[:, rank:] * (1.0 / (full_x * full_y))
    gram = jnp.concatenate([gram, jnp.zeros((count, 128 - count), f32)], axis=1)
    R[8:16] = gram.reshape(8, 8, 128)

    piece = 16 // n_a
    RA[a_me] = R[pl.ds(a_me * piece, piece)]

    def scatter(j):
        m = lax.rem(a_me + j, n_a)
        return pltpu.make_async_remote_copy(
            src_ref=R.at[pl.ds(m * piece, piece)], dst_ref=RA.at[a_me],
            send_sem=as_sem.at[j], recv_sem=ar_sem.at[j],
            device_id=a_device(m), device_id_type=MESH,
        )

    def exchange(j):
        m = lax.rem(b_me + j, n_b)
        return pltpu.make_async_remote_copy(
            src_ref=PB.at[b_me], dst_ref=PB.at[b_me],
            send_sem=ps_sem.at[j], recv_sem=pr_sem.at[j],
            device_id=b_device(m), device_id_type=MESH,
        )

    def gather(j):
        m = lax.rem(a_me + j, n_a)
        return pltpu.make_async_remote_copy(
            src_ref=G.at[a_me], dst_ref=G.at[a_me],
            send_sem=gs_sem.at[j], recv_sem=gr_sem.at[j],
            device_id=a_device(m), device_id_type=MESH,
        )

    def run(make, n):
        @pl.loop(1, n)
        def _(j):
            make(j).start()

        @pl.loop(1, n)
        def _(j):
            make(j).wait_recv()

    def total(ref, n):
        out = ref[0]
        for m in range(1, n):
            out = out + ref[m]
        return out

    run(scatter, n_a)
    PB[b_me] = total(RA, n_a)
    run(exchange, n_b)
    G[a_me] = total(PB, n_b)
    run(gather, n_a)
    whole = G[...].reshape(16, 8, 128)
    coef_out[...] = whole[0:8].reshape(64, 128)
    gram_out[...] = whole[8:16].reshape(64, 128)[:, :64]

    for copy in stores:
        copy.wait()

    @pl.loop(0, STEPS)
    def _(n):
        wait_sends(n)

    @pl.loop(1, n_row)
    def _(j):
        mode_copy(j).wait_send()

    @pl.loop(1, n_a)
    def _(j):
        scatter(j).wait_send()
        gather(j).wait_send()

    @pl.loop(1, n_b)
    def _(j):
        exchange(j).wait_send()


def solution(mesh):
    n_row, n_col = mesh.shape["row"], mesh.shape["col"]
    n_a, n_b = n_row * 2, n_col // 2
    piece = 16 // n_a

    def shards(e_field, h_field, e_coef, basis, pml_width, snap_index):
        nz = e_coef.shape[0]
        rank = basis.shape[0] * n_row
        count = snap_index.shape[0]
        dma = pltpu.SemaphoreType.DMA
        hbm = pl.BlockSpec(memory_space=pl.ANY)
        smem = pl.BlockSpec(memory_space=pltpu.SMEM)
        vmem = pl.BlockSpec(memory_space=pltpu.VMEM)
        planes = pltpu.VMEM((STEPS, 2, nz, 128), f32)
        tiles = pltpu.VMEM((STEPS, 8, 128), f32)
        return pl.pallas_call(
            functools.partial(kernel, n_row, n_col, nz, 3 if nz == 64 else 1),
            out_shape=(
                jax.ShapeDtypeStruct(e_field.shape, f32),
                jax.ShapeDtypeStruct(h_field.shape, f32),
                jax.ShapeDtypeStruct((count, rank), f32),
                jax.ShapeDtypeStruct((count, count), f32),
            ),
            in_specs=[hbm, hbm, hbm, hbm, smem, smem],
            out_specs=(hbm, hbm, vmem, vmem),
            scratch_shapes=[
                pltpu.VMEM((6, nz, 8, 128), f32),
                pltpu.VMEM((nz, 8, 128), f32),
                pltpu.VMEM((8, nz, 8, 128), f32),
                pltpu.VMEM((14, 8, 128), f32),
                planes, planes, tiles, tiles, tiles,
                planes, planes, tiles, tiles, tiles, tiles,
                pltpu.VMEM((rank + count, 8, 128), f32),
                pltpu.VMEM((16, 8, 128), f32),
                pltpu.VMEM((n_a, piece, 8, 128), f32),
                pltpu.VMEM((n_b, piece, 8, 128), f32),
                pltpu.VMEM((n_a, piece, 8, 128), f32),
                dma((3,)), dma((2,)), dma((STEPS, 6)), dma((STEPS, 6)),
                dma((n_row,)), dma((n_row,)), dma((1,)),
                dma((n_a,)), dma((n_a,)), dma((n_b,)), dma((n_b,)), dma((n_a,)), dma((n_a,)),
            ],
            compiler_params=pltpu.CompilerParams(collective_id=0, has_side_effects=True),
            name="yee",
        )(e_field, h_field, e_coef, basis, pml_width, snap_index)

    return jax.shard_map(
        shards,
        mesh=mesh,
        in_specs=(
            P(None, None, "row", "col"),
            P(None, None, "row", "col"),
            P(None, "row", "col"),
            P("row", None, "col"),
            P(),
            P(),
        ),
        out_specs=(P(None, None, "row", "col"), P(None, None, "row", "col"), P(), P()),
        check_vma=False,
    )
```

time: 420 us -> 135 us (0.32)
  Pallas kernels: 0 us -> 130 us
  starting transfers between devices: 119 us -> 0 us
  local copies, waits for them, and re-layouts: 106 us -> 4.41 us
  other arithmetic: 98.7 us -> 0 us
  blocking collectives: 80.6 us -> 0 us
  waiting for transfers between devices: 7.37 us -> 0 us
    pallas_call x0 -> x1, Pallas kernels: none -> 130 us  [shards(): pl.pallas_call(functools.partial(kernel, n_row, n_col, nz, 3 if nz == 64...]
    ppermute x32 -> x0, starting transfers between devices: 112 us -> none  [from_behind(): return lax.ppermute(block, axis, route)]
    psum x5 -> x0, blocking collectives: 80.6 us -> none  [by_axis(): array = lax.psum(array, axis)]
    slice x123 -> x0, local copies, waits for them, and re-layouts: 71.1 us -> none  [the longest x45 33.4 us: forward(): lax.slice_in_dim(field, 1, count, axis=axis)]
    sub x23 -> x0, other arithmetic: 41.8 us -> none  [the longest x8 15.1 us: magnetic(): h_z = h_z - time_step * (ey_dx + psi_hzx - ex_dy - psi_hzy)]
    add x20 -> x0, other arithmetic: 25.6 us -> none  [the longest x6 10.3 us: electric(): e_z = e_z + e_coef * (hy_dx + psi_ezx - hx_dy - psi_ezy)]
    another operation x68 -> x0, local copies, waits for them, and re-layouts: 25.4 us -> none  [the longest x24 12.5 us: forward(): jnp.expand_dims(plane, axis)]
    another operation x23 -> x0, other arithmetic: 10.6 us -> none  [the longest x8 4.32 us: shards(): jnp.stack((h_field[0, :, :, -1], h_field[2, :, :, -1]))]
  transfers between devices with their start and end apart: 33 -> 0, of which waited for: 5 -> 0; matrix products, arithmetic and copies ran while one was open for 38% -> 0% of each run, Pallas kernels for 0% -> 0%
where the time goes in v1:
time: 135 us
  Pallas kernels  130 us (96%)
  local copies, waits for them, and re-layouts  4.41 us (3%)
    pallas_call x1, Pallas kernels, shards(): pl.pallas_call(functools.partial(kernel, n_row, n_col, nz, 3 if nz == 64...  130 us
    unnamed x10, local copies, waits for them, and re-layouts  4.41 us

profile of v1, /device:TPU:1, one launch (start us, length us, event | category | flops | bytes accessed | tf_op | source)
XLA Modules:
  0.0 134.8 jit_solution(12139248382589013133)
XLA Ops:
  0.6 129.8 %yee.1 = (f32[3,64,8,128]{3,2,1,0:T(8,128)}, f32[3,64,8,128]{3,2,1,0:T(8,128)}, f32[64,128]{1,0:T(8,128)}, f32[64,64]{1,0:T(8,128)}) custom-call(f32[3,64,8,128]{3,2,1,0:T(8,128)} %e_in.1, f32[3,64,8,128]{3,2,1,0:T(8,128)} %h_in.1, f32[64,8,128]{2,1,0:T(8,128)} %c_in.1, f32[16,64,128]{2,1,0:T(8,128)} %basis.1, s32[4]{0:T(128)} %pml.1, s32[64]{0:T(128)} %snap.1), custom_call_target="tpu_custom_call" | custom-call | tf_op jit(solution)/shard_map/yee/pallas_call | solution.py:466
  130.4 0.0 copy-start
  130.4 2.1 %copy.14 = f32[3,64,8,128]{3,2,1,0:T(8,128)} copy(f32[3,64,8,128]{3,2,1,0:T(8,128)} %get-tuple-element.8) | data formatting | bytes 1572864
  132.6 0.0 copy-done
  132.6 0.0 copy-start.2
  132.6 0.9 copy.15
  133.5 0.0 copy-done.2
  133.5 0.0 copy-start.1
  133.5 0.6 copy.16
  134.1 0.2 copy-done.1
  134.2 0.6 copy.17
Async XLA Ops:
  130.4 2.1 %copy-start = (f32[3,64,8,128]{3,2,1,0:T(8,128)S(1)}, f32[3,64,8,128]{3,2,1,0:T(8,128)}, u32[]{:S(2)}) copy-start(f32[3,64,8,128]{3,2,1,0:T(8,128)} %get-tuple-element.9) | copy-start | bytes 2359300
  132.6 0.9 copy-start.2
  133.5 0.8 copy-start.1

commit v2 on v1

v2 whole, which is shorter than its diff:
```python
import functools

import jax
import jax.numpy as jnp
from jax import lax
from jax.experimental import pallas as pl
from jax.experimental.pallas import tpu as pltpu
from jax.sharding import PartitionSpec as P

STEPS = 8
time_step = 0.5
sigma_top = 4.0
alpha_shift = 0.05
MESH = pl.DeviceIdType.MESH
TILE = (8, 128)
f32 = jnp.float32


def absorber(positions, total, low, high):
    depth = jnp.maximum(
        jnp.maximum((low - positions) / low, (positions - (total - 1.0 - high)) / high), 0.0
    )
    sigma = sigma_top * (depth * depth * depth)
    damp = jnp.exp(-(sigma + alpha_shift) * time_step)
    gain = sigma / (sigma + alpha_shift) * (damp - 1.0)
    return damp, gain


def kernel(
    n_row, n_col, nz, chunks,
    e_in, h_in, c_in, basis, pml, snap,
    e_out, h_out, coef_out, gram_out,
    F, CE, HP, PSIH, PSIE, K, CAR,
    sxd, sxu, syd, syu, sca, scb,
    rxd, rxu, ryd, ryu, rca, rcb,
    W, M, R, RA, PB, G,
    in_sem, out_sem, hs_sem, hr_sem, bs_sem, br_sem, own_sem,
    as_sem, ar_sem, ps_sem, pr_sem, gs_sem, gr_sem,
):
    pad = STEPS
    deep = -(-(nz + pad) // chunks)
    tall = F.shape[1]
    row = lax.axis_index("row")
    col = lax.axis_index("col")
    n_a, n_b = n_row * 2, n_col // 2
    y_lo = lax.rem(lax.div(col, 2), 2)
    a_me = row * 2 + y_lo
    b_me = lax.div(col, 4) * 2 + lax.rem(col, 2)

    def a_device(m):
        return (lax.div(m, 2), lax.div(col, 4) * 4 + lax.rem(m, 2) * 2 + lax.rem(col, 2))

    def b_device(m):
        return (row, lax.div(m, 2) * 4 + y_lo * 2 + lax.rem(m, 2))

    loads = [
        pltpu.make_async_copy(e_in, F.at[0:3, pad:pad + nz], in_sem.at[0]),
        pltpu.make_async_copy(h_in, F.at[3:6, pad:pad + nz], in_sem.at[1]),
        pltpu.make_async_copy(c_in, CE.at[pad:pad + nz], in_sem.at[2]),
    ]
    for copy in loads:
        copy.start()
    modes_here = basis.shape[0]

    def modes_for(dest):
        return pltpu.make_async_copy(basis.at[:, 8 * dest:8 * dest + 8, :], M.at[dest], own_sem.at[0])

    for dest in range(n_row):
        modes_for(dest).start()

    barrier = pltpu.get_barrier_semaphore()

    def greet(device):
        pl.semaphore_signal(barrier, inc=1, device_id=device, device_id_type=MESH)

    @pl.loop(1, n_a)
    def _(j):
        greet(a_device(lax.rem(a_me + j, n_a)))

    @pl.loop(1, n_b)
    def _(j):
        greet(b_device(lax.rem(b_me + j, n_b)))

    up_x, dn_x = row < n_row - 1, row > 0
    up_y, dn_y = col < n_col - 1, col > 0
    ca_out, ca_in = up_x & dn_y, dn_x & up_y

    @pl.when(up_y)
    def _():
        greet((row, col + 1))

    @pl.when(dn_y)
    def _():
        greet((row, col - 1))

    @pl.when(ca_out)
    def _():
        greet((row + 1, col - 1))

    @pl.when(ca_in)
    def _():
        greet((row - 1, col + 1))

    greeted = n_a - 1 + n_b - 1
    for flag in (up_y, dn_y, ca_out, ca_in):
        greeted = greeted + flag.astype(jnp.int32)

    sub = lax.broadcasted_iota(jnp.int32, TILE, 0)
    lane = lax.broadcasted_iota(jnp.int32, TILE, 1)
    w = [jnp.full(TILE, pml[i], jnp.int32).astype(f32) for i in range(4)]
    x_pos = (row * 8 + sub).astype(f32)
    y_pos = (col * 128 + lane).astype(f32)
    full_x, full_y = float(n_row * 8), float(n_col * 128)
    hdx, hgx = absorber(x_pos + 0.5, full_x, w[0], w[1])
    hdy, hgy = absorber(y_pos + 0.5, full_y, w[2], w[3])
    edx, egx = absorber(x_pos, full_x, w[0], w[1])
    edy, egy = absorber(y_pos, full_y, w[2], w[3])
    _, gxm = absorber((row * 8 - 1 + 0 * sub).astype(f32) + 0.5, full_x, w[0], w[1])
    _, gym = absorber((col * 128 - 1 + 0 * lane).astype(f32) + 0.5, full_y, w[2], w[3])
    s7, s0, l127, l0 = sub == 7, sub == 0, lane == 127, lane == 0
    zero = jnp.zeros(TILE, f32)
    coeffs = [
        hdx, hgx, hdy, hgy, edx, egx, edy, egy,
        jnp.where(s7, 0.5 * (1.0 + hgx), zero), jnp.where(s7, hgx, zero),
        jnp.where(l127, 0.5 * (1.0 + hgy), zero), jnp.where(l127, hgy, zero),
        0.5 * (1.0 + gxm) * dn_x.astype(f32), 0.5 * (1.0 + gym) * dn_y.astype(f32),
    ]
    for i, value in enumerate(coeffs):
        K[i] = value
    HDX, HGX, HDY, HGY, EDX, EGX, EDY, EGY, CXU, PXU, CYU, PYU, CXD, CYD = range(14)

    @pl.loop(0, tall)
    def _(z):
        for i in range(4):
            PSIE[i, z] = zero
            PSIH[i, z] = zero

    for beyond in (*range(pad), *range(pad + nz, tall)):
        CE[beyond] = zero
        for i in range(6):
            F[i, beyond] = zero

    def clear(ref, wanted):
        @pl.when(wanted)
        def _():
            @pl.loop(0, STEPS)
            def _(n):
                ref[n] = jnp.zeros(ref.shape[1:], f32)

    clear(rxd, ~up_x)
    clear(rxu, ~dn_x)
    clear(ryd, ~up_y)
    clear(ryu, ~dn_y)
    clear(rca, ~ca_in)
    clear(rcb, ~ca_out)

    def wide(v):
        return jnp.broadcast_to(v, TILE)

    def roll_l(v, by):
        by = by % 128
        return pltpu.roll(v, by, 1) if by else v

    def roll_s(v, by):
        return pltpu.roll(v, by, 0)

    def partial_h(E, H, psi, ex_next, ey_next):
        ex, ey, ez = E
        hx, hy, hz = H
        ez_dy = jnp.where(l127, 0.0, roll_l(ez, 127)) - ez
        ex_dy = jnp.where(l127, 0.0, roll_l(ex, 127)) - ex
        ez_dx = jnp.where(s7, 0.0, roll_s(ez, 7)) - ez
        ey_dx = jnp.where(s7, 0.0, roll_s(ey, 7)) - ey
        ey_dz = ey_next - ey
        ex_dz = ex_next - ex
        p0, p1, p2, p3 = K[HGY] * ez_dy, K[HGX] * ez_dx, K[HGX] * ey_dx, K[HGY] * ex_dy
        if psi is not None:
            p0, p1 = K[HDY] * psi[0] + p0, K[HDX] * psi[1] + p1
            p2, p3 = K[HDX] * psi[2] + p2, K[HDY] * psi[3] + p3
        hx = hx - time_step * (ez_dy + p0 - ey_dz)
        hy = hy - time_step * (ex_dz - ez_dx - p1)
        hz = hz - time_step * (ey_dx + p2 - ex_dy - p3)
        return (hx, hy, hz), (p0, p1, p2, p3)

    def put(packed, i, low, high):
        if low is not None:
            packed = jnp.where(lane == i, low, packed)
        return jnp.where(lane == 64 + i, high, packed)

    def pack_e(n, c, i, E, pd):
        ex, ey, ez = E
        sxd[n, c, 2 * i:2 * i + 1, :] = ey[0:1, :]
        sxd[n, c, 2 * i + 1:2 * i + 2, :] = ez[0:1, :]
        return put(pd, i, roll_l(ex, i), roll_l(ez, 64 + i))

    def finish_h(n, c, i, z, E, H, later, ex_next, ey_next, pu, pb):
        psi = tuple(PSIH[k, z + pad] for k in range(4)) if later else None
        H, psi = partial_h(E, H, psi, ex_next, ey_next)
        for k in range(3):
            HP[k, z + pad] = H[k]
        for k in range(4):
            PSIH[k, z + pad] = psi[k]
        sxu[n, c, 2 * i:2 * i + 1, :] = H[1][7:8, :]
        sxu[n, c, 2 * i + 1:2 * i + 2, :] = H[2][7:8, :]
        pu = put(pu, i, roll_l(H[0], i - 127), roll_l(H[2], 64 + i - 127))
        pb = put(pb, i, None, roll_l(E[1], 64 + i - 127))
        return pu, pb

    def electric(n, c, i, z, yds, yu, cas, hx_prev, hy_prev):
        p = z + pad
        ex, ey, ez = F[0, p], F[1, p], F[2, p]
        hx, hy, hz = HP[0, p], HP[1, p], HP[2, p]
        p0, p1, p2, p3 = PSIH[0, p], PSIH[1, p], PSIH[2, p], PSIH[3, p]
        if i == 0:
            k, j = lax.max(c - 1, 0), deep - 1
        else:
            k, j = c, i - 1
        yd, ca = yds[i > 0], cas[i > 0]
        ey8 = wide(rxd[n, k, 2 * j:2 * j + 1, :])
        ez8 = wide(rxd[n, k, 2 * j + 1:2 * j + 2, :])
        ex128, ez128 = roll_l(yd, 127 - j), roll_l(yd, 63 - j)
        if i <= pad:
            hx_prev = jnp.where(z == 0, zero, hx_prev)
            hy_prev = jnp.where(z == 0, zero, hy_prev)
        hy = hy + K[CXU] * ez8
        p1 = p1 + K[PXU] * ez8
        hx = hx - K[CYU] * ez128
        p0 = p0 + K[PYU] * ez128
        hz = hz - K[CXU] * ey8 + K[CYU] * ex128
        p2 = p2 + K[PXU] * ey8
        p3 = p3 + K[PYU] * ex128
        hy_m = wide(rxu[n, c, 2 * i:2 * i + 1, :]) + K[CXD] * ez
        hz_m = wide(rxu[n, c, 2 * i + 1:2 * i + 2, :]) - K[CXD] * ey
        hz_m = hz_m + K[CYU] * roll_l(ca, 127 - j)
        hx_w = roll_l(yu, -i) - K[CYD] * ez
        hz_w = roll_l(yu, 64 - i) + K[CYD] * ex
        hz_dy = hz - jnp.where(l0, hz_w, roll_l(hz, 1))
        hx_dy = hx - jnp.where(l0, hx_w, roll_l(hx, 1))
        hz_dx = hz - jnp.where(s0, hz_m, roll_s(hz, 1))
        hy_dx = hy - jnp.where(s0, hy_m, roll_s(hy, 1))
        hy_dz = hy - hy_prev
        hx_dz = hx - hx_prev
        q0 = K[EDY] * PSIE[0, p] + K[EGY] * hz_dy
        q1 = K[EDX] * PSIE[1, p] + K[EGX] * hz_dx
        q2 = K[EDX] * PSIE[2, p] + K[EGX] * hy_dx
        q3 = K[EDY] * PSIE[3, p] + K[EGY] * hx_dy
        PSIE[0, p], PSIE[1, p], PSIE[2, p], PSIE[3, p] = q0, q1, q2, q3
        ce = CE[p]
        ex = ex + ce * (hz_dy + q0 - hy_dz)
        ey = ey + ce * (hx_dz - hz_dx - q1)
        ez = ez + ce * (hy_dx + q2 - hx_dy - q3)
        F[0, p], F[1, p], F[2, p] = ex, ey, ez
        PSIH[0, p], PSIH[1, p], PSIH[2, p], PSIH[3, p] = p0, p1, p2, p3
        return (ex, ey, ez), (hx, hy, hz)

    routes = [
        (dn_x, up_x, sxd, rxd, (row - 1, col)),
        (up_x, dn_x, sxu, rxu, (row + 1, col)),
        (dn_y, up_y, syd, ryd, (row, col - 1)),
        (up_y, dn_y, syu, ryu, (row, col + 1)),
        (ca_out, ca_in, sca, rca, (row + 1, col - 1)),
        (ca_in, ca_out, scb, rcb, (row - 1, col + 1)),
    ]

    def message(i, n, c):
        _, _, src, dst, device = routes[i]
        return pltpu.make_async_remote_copy(
            src_ref=src.at[n, c], dst_ref=dst.at[n, c],
            send_sem=hs_sem.at[i], recv_sem=hr_sem.at[lax.rem(n, 2), c, i],
            device_id=device, device_id_type=MESH,
        )

    def arrived(n, c):
        for i in range(6):
            pl.when(routes[i][1])(lambda: message(i, n, c).wait_recv())
        before = lax.max(c - 1, 0)
        yu = ryu[n, c] - K[CXU] * wide(rcb[n, c])
        cas = wide(rca[n, before]), wide(rca[n, c])
        return (ryd[n, before], ryd[n, c]), yu, cas

    def send(n, c, pd, pu, pb):
        syd[n, c], syu[n, c], sca[n, c], scb[n, c] = pd, pu, pd[7:8, :], pb[0:1, :]
        for i in (4, 5, 0, 1, 2, 3):
            pl.when(routes[i][0])(lambda: message(i, n, c).start())

    def bytes_of(ref, sem):
        pltpu.make_async_copy(ref, ref, sem).wait()

    def all_left():
        for i in range(6):
            pl.when(routes[i][0])(lambda: bytes_of(routes[i][2], hs_sem.at[i]))

    def mode_copy(j, first, count):
        dest = lax.rem(row + j, n_row)
        return pltpu.make_async_remote_copy(
            src_ref=M.at[dest, pl.ds(first, count)],
            dst_ref=W.at[pl.ds(row * modes_here + first, count)],
            send_sem=bs_sem.at[0], recv_sem=br_sem.at[0],
            device_id=(dest, col), device_id_type=MESH,
        )

    def mode_piece(k):
        half = modes_here // 2
        mode_copy(1 + 2 * lax.div(k, 2), lax.rem(k, 2) * half, half).start()

    for copy in loads:
        copy.wait()
    pl.semaphore_wait(barrier, greeted)
    none = (zero, zero, zero)

    def opening(c, carry):
        E, H = carry
        pd = pu = pb = zero
        for i in range(deep):
            z = c * deep + i
            p = z + pad
            ahead = F[0, p], F[1, p], F[2, p]
            pd = pack_e(0, c, i, ahead, pd)
            pu, pb = finish_h(0, c, i, z - 1, E, H, False, ahead[0], ahead[1], pu, pb)
            E, H = ahead, (F[3, p], F[4, p], F[5, p])
        send(0, c, pd, pu, pb)
        return E, H

    lax.fori_loop(0, chunks, opening, (none, none))
    for k in range(3):
        CAR[k] = zero
    bytes_of(M, own_sem.at[0])
    for j in range(2, n_row, 2):
        mode_copy(j, 0, modes_here).start()
    mode_piece(n_row - 1)

    @pl.loop(0, STEPS - 1)
    def _(n):
        @pl.when(n < n_row - 1)
        def _():
            mode_piece(n)

        @pl.loop(0, chunks)
        def _(c):
            yds, yu, cas = arrived(n, c)
            pd = pu = pb = zero
            below = c * deep - (n + 2) + pad
            E = F[0, below], F[1, below], F[2, below]
            H = CAR[0], CAR[1], CAR[2]
            for i in range(deep):
                z = c * deep - (n + 1) + i
                E2, H2 = electric(n, c, i, z, yds, yu, cas, H[0], H[1])
                pd = pack_e(n + 1, c, i, E2, pd)
                pu, pb = finish_h(n + 1, c, i, z - 1, E, H, True, E2[0], E2[1], pu, pb)
                E, H = E2, H2
            for k, value in enumerate(H):
                CAR[k] = value
            send(n + 1, c, pd, pu, pb)

    def closing(c, carry):
        n = STEPS - 1
        yds, yu, cas = arrived(n, c)
        for i in range(deep):
            z = c * deep - (n + 1) + i
            _, H = electric(n, c, i, z, yds, yu, cas, carry[0], carry[1])
            F[3, z + pad], F[4, z + pad], F[5, z + pad] = H
            carry = H[0], H[1]
        return carry

    lax.fori_loop(0, chunks, closing, (zero, zero))

    stores = [
        pltpu.make_async_copy(F.at[0:3, pad:pad + nz], e_out, out_sem.at[0]),
        pltpu.make_async_copy(F.at[3:6, pad:pad + nz], h_out, out_sem.at[1]),
    ]
    for copy in stores:
        copy.start()

    count = snap.shape[0]
    rank = modes_here * n_row

    @pl.loop(0, count // 8)
    def _(g):
        for k in range(8):
            plane = snap[g * 8 + k]
            W[rank + g * 8 + k] = F[lax.div(plane, nz), pad + lax.rem(plane, nz)]

    W[pl.ds(row * modes_here, modes_here)] = M[row]

    elsewhere = W.at[0:rank - modes_here]
    bytes_of(elsewhere, br_sem.at[0])

    both = jnp.zeros((count, rank + count), f32)
    for x in range(8):
        both = both + lax.dot_general(
            W[rank:rank + count, x, :], W[:, x, :], (((1,), (1,)), ((), ())),
            precision=lax.Precision.HIGHEST, preferred_element_type=f32,
        )
    R[0:8] = both[:, :rank].reshape(8, 8, 128)
    gram = both[:, rank:] * (1.0 / (full_x * full_y))
    gram = jnp.concatenate([gram, jnp.zeros((count, 128 - count), f32)], axis=1)
    R[8:16] = gram.reshape(8, 8, 128)

    piece = 16 // n_a
    RA[a_me] = R[pl.ds(a_me * piece, piece)]

    def scatter(j):
        m = lax.rem(a_me + j, n_a)
        return pltpu.make_async_remote_copy(
            src_ref=R.at[pl.ds(m * piece, piece)], dst_ref=RA.at[a_me],
            send_sem=as_sem.at[0], recv_sem=ar_sem.at[0],
            device_id=a_device(m), device_id_type=MESH,
        )

    def exchange(j):
        m = lax.rem(b_me + j, n_b)
        return pltpu.make_async_remote_copy(
            src_ref=PB.at[b_me], dst_ref=PB.at[b_me],
            send_sem=ps_sem.at[0], recv_sem=pr_sem.at[0],
            device_id=b_device(m), device_id_type=MESH,
        )

    def gather(j):
        m = lax.rem(a_me + j, n_a)
        return pltpu.make_async_remote_copy(
            src_ref=G.at[a_me], dst_ref=G.at[a_me],
            send_sem=gs_sem.at[0], recv_sem=gr_sem.at[0],
            device_id=a_device(m), device_id_type=MESH,
        )

    def run(make, n, land, sem, meanwhile=None):
        @pl.loop(1, n)
        def _(j):
            make(j).start()

        if meanwhile is not None:
            meanwhile()
        bytes_of(land.at[0:n - 1], sem.at[0])

    def total(ref, n):
        out = ref[0]
        for m in range(1, n):
            out = out + ref[m]
        return out

    run(scatter, n_a, RA, ar_sem, all_left)
    PB[b_me] = total(RA, n_a)
    run(exchange, n_b, PB, pr_sem)
    G[a_me] = total(PB, n_b)
    run(gather, n_a, G, gr_sem)
    whole = G[...].reshape(16, 8, 128)
    coef_out[...] = whole[0:8].reshape(64, 128)
    gram_out[...] = whole[8:16].reshape(64, 128)[:, :64]

    for copy in stores:
        copy.wait()

    bytes_of(elsewhere, bs_sem.at[0])
    bytes_of(RA.at[0:n_a - 1], as_sem.at[0])
    bytes_of(PB.at[0:n_b - 1], ps_sem.at[0])
    bytes_of(G.at[0:n_a - 1], gs_sem.at[0])


def solution(mesh):
    n_row, n_col = mesh.shape["row"], mesh.shape["col"]
    n_a, n_b = n_row * 2, n_col // 2
    piece = 16 // n_a

    def shards(e_field, h_field, e_coef, basis, pml_width, snap_index):
        nz = e_coef.shape[0]
        rank = basis.shape[0] * n_row
        count = snap_index.shape[0]
        dma = pltpu.SemaphoreType.DMA
        hbm = pl.BlockSpec(memory_space=pl.ANY)
        smem = pl.BlockSpec(memory_space=pltpu.SMEM)
        vmem = pl.BlockSpec(memory_space=pltpu.VMEM)
        chunks = 6 if nz == 64 else 2
        deep = -(-(nz + STEPS) // chunks)
        tall = deep * chunks + STEPS
        rows = pltpu.VMEM((STEPS, chunks, -(-deep // 4) * 8, 128), f32)
        tiles = pltpu.VMEM((STEPS, chunks, 8, 128), f32)
        lines = pltpu.VMEM((STEPS, chunks, 1, 128), f32)
        return pl.pallas_call(
            functools.partial(kernel, n_row, n_col, nz, chunks),
            out_shape=(
                jax.ShapeDtypeStruct(e_field.shape, f32),
                jax.ShapeDtypeStruct(h_field.shape, f32),
                jax.ShapeDtypeStruct((count, rank), f32),
                jax.ShapeDtypeStruct((count, count), f32),
            ),
            in_specs=[hbm, hbm, hbm, hbm, smem, smem],
            out_specs=(hbm, hbm, vmem, vmem),
            scratch_shapes=[
                pltpu.VMEM((6, tall, 8, 128), f32),
                pltpu.VMEM((tall, 8, 128), f32),
                pltpu.VMEM((3, tall, 8, 128), f32),
                pltpu.VMEM((4, tall, 8, 128), f32),
                pltpu.VMEM((4, tall, 8, 128), f32),
                pltpu.VMEM((14, 8, 128), f32),
                pltpu.VMEM((3, 8, 128), f32),
                rows, rows, tiles, tiles, lines, lines,
                rows, rows, tiles, tiles, lines, lines,
                pltpu.VMEM((rank + count, 8, 128), f32),
                pltpu.VMEM((n_row, basis.shape[0], 8, 128), f32),
                pltpu.VMEM((16, 8, 128), f32),
                pltpu.VMEM((n_a, piece, 8, 128), f32),
                pltpu.VMEM((n_b, piece, 8, 128), f32),
                pltpu.VMEM((n_a, piece, 8, 128), f32),
                dma((3,)), dma((2,)), dma((6,)), dma((2, chunks, 6)),
                dma((1,)), dma((1,)), dma((1,)),
                dma((1,)), dma((1,)), dma((1,)), dma((1,)), dma((1,)), dma((1,)),
            ],
            compiler_params=pltpu.CompilerParams(collective_id=0, has_side_effects=True),
            name="yee",
        )(e_field, h_field, e_coef, basis, pml_width, snap_index)

    return jax.shard_map(
        shards,
        mesh=mesh,
        in_specs=(
            P(None, None, "row", "col"),
            P(None, None, "row", "col"),
            P(None, "row", "col"),
            P("row", None, "col"),
            P(),
            P(),
        ),
        out_specs=(P(None, None, "row", "col"), P(None, None, "row", "col"), P(), P()),
        check_vma=False,
    )
```

time: 135 us -> 77.3 us (0.57)
  Pallas kernels: 130 us -> 72 us
    pallas_call x1, Pallas kernels: 130 us -> 72 us  [shards(): pl.pallas_call(functools.partial(kernel, n_row, n_col, nz, chunks), out_s...]
where the time goes in v2:
time: 77.3 us; the launch traced here: 77 us
  Pallas kernels  72 us (93%)
  local copies, waits for them, and re-layouts  4.41 us (6%)
    pallas_call x1, Pallas kernels, shards(): pl.pallas_call(functools.partial(kernel, n_row, n_col, nz, chunks), out_s...  72 us
    unnamed x10, local copies, waits for them, and re-layouts  4.41 us

profile of v2, /device:TPU:1, one launch (start us, length us, event | category | flops | bytes accessed | tf_op | source)
XLA Modules:
  0.0 77.0 jit_solution(16087149147654428984)
XLA Ops:
  0.6 72.0 %yee.1 = (f32[3,64,8,128]{3,2,1,0:T(8,128)}, f32[3,64,8,128]{3,2,1,0:T(8,128)}, f32[64,128]{1,0:T(8,128)}, f32[64,64]{1,0:T(8,128)}) custom-call(f32[3,64,8,128]{3,2,1,0:T(8,128)} %e_in.1, f32[3,64,8,128]{3,2,1,0:T(8,128)} %h_in.1, f32[64,8,128]{2,1,0:T(8,128)} %c_in.1, f32[16,64,128]{2,1,0:T(8,128)} %basis.1, s32[4]{0:T(128)} %pml.1, s32[64]{0:T(128)} %snap.1), custom_call_target="tpu_custom_call" | custom-call | tf_op jit(solution)/shard_map/yee/pallas_call | solution.py:478
  72.6 0.0 copy-start
  72.6 2.1 %copy.14 = f32[3,64,8,128]{3,2,1,0:T(8,128)} copy(f32[3,64,8,128]{3,2,1,0:T(8,128)} %get-tuple-element.8) | data formatting | bytes 1572864
  74.8 0.0 copy-done
  74.8 0.0 copy-start.2
  74.8 0.9 %copy.15 = f32[3,64,8,128]{3,2,1,0:T(8,128)} copy(f32[3,64,8,128]{3,2,1,0:T(8,128)S(1)} %copy-done) | data formatting | bytes 1572864
  75.7 0.0 copy-done.2
  75.7 0.0 copy-start.1
  75.7 0.6 copy.16
  76.3 0.2 copy-done.1
  76.4 0.6 copy.17
Async XLA Ops:
  72.6 2.1 %copy-start = (f32[3,64,8,128]{3,2,1,0:T(8,128)S(1)}, f32[3,64,8,128]{3,2,1,0:T(8,128)}, u32[]{:S(2)}) copy-start(f32[3,64,8,128]{3,2,1,0:T(8,128)} %get-tuple-element.9) | copy-start | bytes 2359300
  74.8 0.9 %copy-start.2 = (f32[64,128]{1,0:T(8,128)S(1)}, f32[64,128]{1,0:T(8,128)}, u32[]{:S(2)}) copy-start(f32[64,128]{1,0:T(8,128)} %get-tuple-element.10) | copy-start | bytes 98308
  75.7 0.8 %copy-start.1 = (f32[64,64]{1,0:T(8,128)S(1)}, f32[64,64]{1,0:T(8,128)}, u32[]{:S(2)}) copy-start(f32[64,64]{1,0:T(8,128)} %get-tuple-element.11) | copy-start | bytes 49156

commit v3 on v2

--- a/solution.py
+++ b/solution.py
@@ -29,12 +29,12 @@
 def kernel(
     n_row, n_col, nz, chunks,
     e_in, h_in, c_in, basis, pml, snap,
-    e_out, h_out, coef_out, gram_out,
-    F, CE, HP, PSIH, PSIE, K, CAR,
+    F, coef_out, gram_out,
+    CE, HP, PSIH, PSIE, K, CAR,
     sxd, sxu, syd, syu, sca, scb,
     rxd, rxu, ryd, ryu, rca, rcb,
     W, M, R, RA, PB, G,
-    in_sem, out_sem, hs_sem, hr_sem, bs_sem, br_sem, own_sem,
+    in_sem, hs_sem, hr_sem, bs_sem, br_sem, own_sem,
     as_sem, ar_sem, ps_sem, pr_sem, gs_sem, gr_sem,
 ):
     pad = STEPS
@@ -364,13 +364,6 @@
 
     lax.fori_loop(0, chunks, closing, (zero, zero))
 
-    stores = [
-        pltpu.make_async_copy(F.at[0:3, pad:pad + nz], e_out, out_sem.at[0]),
-        pltpu.make_async_copy(F.at[3:6, pad:pad + nz], h_out, out_sem.at[1]),
-    ]
-    for copy in stores:
-        copy.start()
-
     count = snap.shape[0]
     rank = modes_here * n_row
 
@@ -447,8 +440,6 @@
     coef_out[...] = whole[0:8].reshape(64, 128)
     gram_out[...] = whole[8:16].reshape(64, 128)[:, :64]
 
-    for copy in stores:
-        copy.wait()
 
     bytes_of(elsewhere, bs_sem.at[0])
     bytes_of(RA.at[0:n_a - 1], as_sem.at[0])
@@ -475,18 +466,16 @@
         rows = pltpu.VMEM((STEPS, chunks, -(-deep // 4) * 8, 128), f32)
         tiles = pltpu.VMEM((STEPS, chunks, 8, 128), f32)
         lines = pltpu.VMEM((STEPS, chunks, 1, 128), f32)
-        return pl.pallas_call(
+        fields, coefficients, gram = pl.pallas_call(
             functools.partial(kernel, n_row, n_col, nz, chunks),
             out_shape=(
-                jax.ShapeDtypeStruct(e_field.shape, f32),
-                jax.ShapeDtypeStruct(h_field.shape, f32),
-                jax.ShapeDtypeStruct((count, rank), f32),
-                jax.ShapeDtypeStruct((count, count), f32),
+                pltpu.VMEM((6, tall, 8, 128), f32),
+                pltpu.VMEM((count, rank), f32),
+                pltpu.VMEM((count, count), f32),
             ),
             in_specs=[hbm, hbm, hbm, hbm, smem, smem],
-            out_specs=(hbm, hbm, vmem, vmem),
+            out_specs=(vmem, vmem, vmem),
             scratch_shapes=[
-                pltpu.VMEM((6, tall, 8, 128), f32),
                 pltpu.VMEM((tall, 8, 128), f32),
                 pltpu.VMEM((3, tall, 8, 128), f32),
                 pltpu.VMEM((4, tall, 8, 128), f32),
@@ -501,13 +490,40 @@
                 pltpu.VMEM((n_a, piece, 8, 128), f32),
                 pltpu.VMEM((n_b, piece, 8, 128), f32),
                 pltpu.VMEM((n_a, piece, 8, 128), f32),
-                dma((3,)), dma((2,)), dma((6,)), dma((2, chunks, 6)),
+                dma((3,)), dma((6,)), dma((2, chunks, 6)),
                 dma((1,)), dma((1,)), dma((1,)),
                 dma((1,)), dma((1,)), dma((1,)), dma((1,)), dma((1,)), dma((1,)),
             ],
             compiler_params=pltpu.CompilerParams(collective_id=0, has_side_effects=True),
             name="yee",
         )(e_field, h_field, e_coef, basis, pml_width, snap_index)
+
+        def write(F, coef, gram, e_out, h_out, coef_out, gram_out, sem):
+            inner = slice(STEPS, STEPS + nz)
+            copies = [
+                pltpu.make_async_copy(F.at[0:3, inner], e_out, sem.at[0]),
+                pltpu.make_async_copy(F.at[3:6, inner], h_out, sem.at[1]),
+                pltpu.make_async_copy(coef, coef_out, sem.at[2]),
+                pltpu.make_async_copy(gram, gram_out, sem.at[3]),
+            ]
+            for copy in copies:
+                copy.start()
+            for copy in copies:
+                copy.wait()
+
+        return pl.pallas_call(
+            write,
+            out_shape=(
+                jax.ShapeDtypeStruct(e_field.shape, f32),
+                jax.ShapeDtypeStruct(h_field.shape, f32),
+                jax.ShapeDtypeStruct((count, rank), f32),
+                jax.ShapeDtypeStruct((count, count), f32),
+            ),
+            in_specs=[vmem, vmem, vmem],
+            out_specs=(hbm, hbm, hbm, hbm),
+            scratch_shapes=[dma((4,))],
+            name="write",
+        )(*[pltpu.with_memory_space_constraint(v, pltpu.VMEM) for v in (fields, coefficients, gram)])
 
     return jax.shard_map(
         shards,

time: 77.3 us -> 73.6 us (0.952)
  local copies, waits for them, and re-layouts: 4.41 us -> 0 us
  Pallas kernels: 72 us -> 72.9 us
    unnamed x10 -> x0, local copies, waits for them, and re-layouts: 4.41 us -> none
    pallas_call x0 -> x1, Pallas kernels: none -> 1.18 us  [shards(): pl.pallas_call(write, out_shape=(jax.ShapeDtypeStruct(e_field.shape, f32)...]
where the time goes in v3:
time: 73.6 us; the launch traced here: 73.5 us
  Pallas kernels  72.9 us (99%)
    pallas_call x1, Pallas kernels, shards(): pl.pallas_call(functools.partial(kernel, n_row, n_col, nz, chunks), out_s...  71.7 us

profile of v3, /device:TPU:1, one launch (start us, length us, event | category | flops | bytes accessed | tf_op | source)
XLA Modules:
  0.0 73.5 jit_solution(4002226563379035704)
XLA Ops:
  0.6 71.7 %yee.1 = (f32[6,80,8,128]{3,2,1,0:T(8,128)S(1)}, f32[64,128]{1,0:T(8,128)S(1)}, f32[64,64]{1,0:T(8,128)S(1)}) custom-call(f32[3,64,8,128]{3,2,1,0:T(8,128)} %e_in.1, f32[3,64,8,128]{3,2,1,0:T(8,128)} %h_in.1, f32[64,8,128]{2,1,0:T(8,128)} %c_in.1, f32[16,64,128]{2,1,0:T(8,128)} %basis.1, s32[4]{0:T(128)} %pml.1, s32[64]{0:T(128)} %snap.1), custom_call_target="tpu_custom_call" | custom-call | tf_op jit(solution)/shard_map/yee/pallas_call | solution.py:469
  72.3 1.2 %write.1 = (f32[3,64,8,128]{3,2,1,0:T(8,128)}, f32[3,64,8,128]{3,2,1,0:T(8,128)}, f32[64,128]{1,0:T(8,128)}, f32[64,64]{1,0:T(8,128)}) custom-call(f32[6,80,8,128]{3,2,1,0:T(8,128)S(1)} %get-tuple-element.7.F, f32[64,128]{1,0:T(8,128)S(1)} %get-tuple-element.8.coef, f32[64,64]{1,0:T(8,128)S(1)} %get-tuple-element.9.gram), custom_call_target="tpu_custom_call" | custom-call | tf_op jit(solution)/shard_map/write/pallas_call | solution.py:514

commit v4 on v3

--- a/solution.py
+++ b/solution.py
@@ -300,8 +300,8 @@
         )
 
     def mode_piece(k):
-        half = modes_here // 2
-        mode_copy(1 + 2 * lax.div(k, 2), lax.rem(k, 2) * half, half).start()
+        part = modes_here // 4
+        mode_copy(1 + 2 * lax.div(k, 4), lax.rem(k, 4) * part, part).start()
 
     for copy in loads:
         copy.wait()
@@ -327,13 +327,11 @@
     bytes_of(M, own_sem.at[0])
     for j in range(2, n_row, 2):
         mode_copy(j, 0, modes_here).start()
-    mode_piece(n_row - 1)
+    mode_piece(2 * n_row - 2)
+    mode_piece(2 * n_row - 1)
 
     @pl.loop(0, STEPS - 1)
     def _(n):
-        @pl.when(n < n_row - 1)
-        def _():
-            mode_piece(n)
 
         @pl.loop(0, chunks)
         def _(c):
@@ -351,6 +349,10 @@
             for k, value in enumerate(H):
                 CAR[k] = value
             send(n + 1, c, pd, pu, pb)
+
+            @pl.when(lax.rem(c, 3) == 2)
+            def _():
+                mode_piece(2 * n + lax.div(c, 3))
 
     def closing(c, carry):
         n = STEPS - 1

time: 73.6 us -> 73.2 us (level)
  no operation moved by 1% of the time
where the time goes in v4:
time: 73.2 us; the launch traced here: 73 us
  Pallas kernels  72.4 us (99%)
    pallas_call x1, Pallas kernels, shards(): pl.pallas_call(functools.partial(kernel, n_row, n_col, nz, chunks), out_s...  71.2 us

profile of v4, /device:TPU:1, one launch (start us, length us, event | category | flops | bytes accessed | tf_op | source)
XLA Modules:
  0.0 73.0 jit_solution(10716672183317565300)
XLA Ops:
  0.6 71.2 %yee.1 = (f32[6,80,8,128]{3,2,1,0:T(8,128)S(1)}, f32[64,128]{1,0:T(8,128)S(1)}, f32[64,64]{1,0:T(8,128)S(1)}) custom-call(f32[3,64,8,128]{3,2,1,0:T(8,128)} %e_in.1, f32[3,64,8,128]{3,2,1,0:T(8,128)} %h_in.1, f32[64,8,128]{2,1,0:T(8,128)} %c_in.1, f32[16,64,128]{2,1,0:T(8,128)} %basis.1, s32[4]{0:T(128)} %pml.1, s32[64]{0:T(128)} %snap.1), custom_call_target="tpu_custom_call" | custom-call | tf_op jit(solution)/shard_map/yee/pallas_call | solution.py:471
  71.8 1.2 %write.1 = (f32[3,64,8,128]{3,2,1,0:T(8,128)}, f32[3,64,8,128]{3,2,1,0:T(8,128)}, f32[64,128]{1,0:T(8,128)}, f32[64,64]{1,0:T(8,128)}) custom-call(f32[6,80,8,128]{3,2,1,0:T(8,128)S(1)} %get-tuple-element.7.F, f32[64,128]{1,0:T(8,128)S(1)} %get-tuple-element.8.coef, f32[64,64]{1,0:T(8,128)S(1)} %get-tuple-element.9.gram), custom_call_target="tpu_custom_call" | custom-call | tf_op jit(solution)/shard_map/write/pallas_call | solution.py:516
